TPU v7x, 32 devices: a whole 2x2x4 slice. The times are simulated.
32 devices in a mesh: tier: 4 (over y, core), mode: 8 (over z, x).
Axes of the slice: x: 2, y: 2, z: 4, core: 2. Of those that a mesh axis runs over, the one named last changes fastest.
Arguments:
- ados: float32 [4, 8, 2, 2, 9216], P('tier', 'mode'), may hold values from -6 to 6
- hamiltonian: float32 [96, 96], replicated, may hold values from -0.3125 to 0.3125
- couplings: float32 [16, 96], replicated, may hold values from -2.4 to 2.4
- rates: float32 [16], replicated, may hold values from 0.05 to 0.6
- strength: float32 [2, 16], replicated, may hold values from -1.8 to 1.8
- occupancy: int32 [4, 8, 2, 16], P('tier', 'mode'), may hold values from 0 to 8, as said below
- up_index: int32 [4, 8, 2, 16], P('tier', 'mode'), may hold values from 0 to 8, as said below
- down_index: int32 [4, 8, 2, 16], P('tier', 'mode'), may hold values from 0 to 8, as said below
Outputs:
- evolved: float32 [4, 8, 2, 2, 9216], P('tier', 'mode')
Inputs may be any that keep to these rules, and one draw needn't show every extreme that they name: `occupancy`: each matrix is occupied in at most 8 quanta in all, summed over the 16 modes; higher tier bins hold matrices of higher tiers on average. For each mode, up_index and down_index describe the same pairs in the two directions: if the entry of matrix a for mode k in up_index names matrix b, then the entry of b for mode k in down_index names a, and the reverse; no matrix is named twice for one mode. The value 4 * 2 names no matrix, and no entry names a tier outside the hierarchy. `down_index`: see up_index.
All inputs are finite; a program needn't handle non-finite values.
Results may differ from a plain program's by a relative error of at most 0.00005.
Values sent between devices are 32-bit elements; how exact they have to be, the bound alone decides.
No kernel may reach another device: no remote copies, remote signals or barrier semaphores. Data moves between devices by JAX's collectives and lax.ppermute only.
A program may use at most 64 MiB of HBM per device.

v0:
```python
import functools

import jax
import jax.numpy as jnp
import numpy as np
from jax import lax
from jax.experimental import pallas as pl
from jax.experimental.pallas import tpu as pltpu
from jax.sharding import PartitionSpec as P

TIME_STEP = 0.3
HIGHEST = lax.Precision.HIGHEST
AXES = ("tier", "mode")


def swap_pairs(pairs):
    return [route for a, b in pairs for route in ((a, b), (b, a))]


def routes(tiers, modes):
    def at(tier, mode):
        return tier * modes + mode % modes

    chips = tiers // 2
    core = [(at(2 * y, m), at(2 * y + 1, m)) for y in range(chips) for m in range(modes)]
    mode = [[(at(t, m), at(t, m + 1)) for t in range(tiers) for m in range(p, modes, 2)] for p in (0, 1)]
    flat, slant = [], []
    for p in (0, 1):
        lower = range(p, chips - 1, 2)
        flat.append([(at(2 * y + c, m), at(2 * y + 2 + c, m)) for y in lower for c in (0, 1) for m in range(modes)])
        slant.append([(at(2 * y + c, m), at(2 * y + 2 + c, m + 1)) for y in lower for c in (0, 1) for m in range(modes)])
    return (
        swap_pairs(core),
        [swap_pairs(r) for r in mode],
        [swap_pairs(r) for r in flat],
        [swap_pairs(r) for r in slant],
    )


def block_plan(groups, slots):
    blocks = groups * slots * 2
    rows = []
    for k in range(blocks):
        for e in range(blocks):
            d = (e + k) % blocks
            dest, source = d // 2, e // 2
            rows.append((dest, source % slots, source // slots - dest // slots, d % 2, e % 2, float(d == e)))
    return np.array(rows, np.float32)


def weights_of(plan, info, base, rise, role_up, role_down, flip, strength, slots):
    modes = strength.shape[1]
    dest = plan[:, 0].astype(np.int32)
    pick = np.eye(info.shape[0], dtype=np.float32)[dest]
    local = jnp.dot(pick, info, precision=HIGHEST)
    level, up, down = local[:, :modes], local[:, modes : 2 * modes], local[:, 2 * modes :]
    same = (plan[:, 2:3] == 0).astype(np.float32)
    name = (base + rise * (1 - same)) * slots + plan[:, 1:2]
    climb = plan[:, 2:3] * flip
    go_up = role_up * jnp.maximum(same, (climb == 1).astype(jnp.float32))
    go_down = role_down * jnp.maximum(same, (climb == -1).astype(jnp.float32))
    ups = go_up * (up == name)
    downs = go_down * (down == name) * level
    gap = ups + downs * strength[0][None, :]
    plus = downs * strength[1][None, :]
    straight = plan[:, 3:4] == plan[:, 4:5]
    sign = plan[:, 4:5] - plan[:, 3:4]
    return jnp.where(straight, plus, sign * gap), jnp.where(straight, plus, -sign * gap), level


def table_of(row_part, column_part, blocks, width):
    spread = np.kron(np.eye(blocks, dtype=np.float32), np.ones((1, width), np.float32))
    groups = row_part.shape[0] // blocks
    rows = row_part.reshape(groups, blocks, -1)
    wide = jnp.einsum("gea,el->gal", rows, spread, precision=HIGHEST)
    return wide + column_part.reshape(groups, 1, blocks * width)


def turned(value, steps, width):
    return value if steps == 0 else pltpu.roll(value, steps * width, 1)


def swapped(value):
    half = value.shape[1] // 2
    return jnp.concatenate([value[:, half:], value[:, :half]], 1)


def own_kernel(step, width, w_ref, other_ref, start_ref, near_ref, far_ref, right_ref, table_ref, out_ref, comm_ref):
    rows, lanes = w_ref.shape
    half = lanes // 2
    w = w_ref[...]
    left = jnp.dot(near_ref[...], w, precision=HIGHEST, preferred_element_type=jnp.float32)
    left += jnp.dot(far_ref[...], other_ref[...], precision=HIGHEST, preferred_element_type=jnp.float32)
    stacked = jnp.concatenate([w[:, :half], w[:, half:]], 0)
    right = jnp.dot(stacked, right_ref[...], precision=HIGHEST, preferred_element_type=jnp.float32)
    comm_ref[:, :half] = left[:, :half] - right[:rows]
    comm_ref[:, half:] = left[:, half:] - right[rows:]
    blocks = table_ref.shape[0]
    odd = (lax.broadcasted_iota(jnp.int32, (8, lanes), 1) // width) % 2 == 1
    for at in range(0, rows, 8):
        part = pl.ds(at, 8)
        value, comm = w_ref[part, :], comm_ref[part, :]
        total = None
        for k in range(blocks // 2):
            near = table_ref[k, part, :] * value
            far = table_ref[k + blocks // 2, part, :] * value
            if k == 1:
                near += jnp.where(odd, 0.0, -comm)
            if k + blocks // 2 == blocks - 1:
                far += jnp.where(odd, comm, 0.0)
            piece = turned(near + swapped(far), k, width)
            total = piece if total is None else total + piece
        out_ref[part, :] = start_ref[part, :] + step * total


def link_kernel(step, width, edges, *refs):
    part_ref, x_ref, z_ref, x_table, z_table = refs[:5]
    edge_refs = refs[5 : 5 + 4 * len(edges)]
    out_ref = refs[5 + 4 * len(edges)]
    edge_out = refs[6 + 4 * len(edges) :]
    rows, lanes = part_ref.shape
    half = lanes // 2
    blocks = x_table.shape[0]
    for at in range(0, rows, 8):
        part = pl.ds(at, 8)
        x, z = x_ref[part, :], z_ref[part, :]
        total = None
        for k in range(blocks // 2):
            near = x_table[k, part, :] * x + z_table[k, part, :] * z
            k_far = k + blocks // 2
            far = x_table[k_far, part, :] * x + z_table[k_far, part, :] * z
            piece = turned(near + swapped(far), k, width)
            total = piece if total is None else total + piece
        halves = [total[:, :half], total[:, half:]]
        for n, place in enumerate(edges):
            flat, slant, flat_table, slant_table = edge_refs[4 * n : 4 * n + 4]
            a, b = flat[part, :], slant[part, :]
            for k in range(blocks // 2):
                piece = flat_table[k, part, :] * a + slant_table[k, part, :] * b
                halves[place] = halves[place] + turned(piece, k, width)
        new = [part_ref[part, :half] + step * halves[0], part_ref[part, half:] + step * halves[1]]
        out_ref[part, :half] = new[0]
        out_ref[part, half:] = new[1]
        for n, place in enumerate(edges[: len(edge_out)]):
            edge_out[n][part, :] = new[place]


VMEM = pl.BlockSpec(memory_space=pltpu.VMEM)


def shards(tiers, modes, ados, hamiltonian, couplings, rates, strength, occupancy, up_index, down_index):
    core_route, mode_routes, flat_routes, slant_routes = routes(tiers, modes)
    slots, size = ados.shape[2], hamiltonian.shape[0]
    half, lanes = size // 2, slots * 2 * size
    tier, mode = lax.axis_index("tier"), lax.axis_index("mode")
    core, chip = tier % 2, tier // 2
    turn = chip % 2
    place = core ^ turn

    def send(value, route):
        return lax.ppermute(value, AXES, route)

    own = ados.reshape(slots * 2, size, size).transpose(1, 0, 2).reshape(size, lanes)
    keep = lax.dynamic_slice(own, (core * half, 0), (half, lanes))
    got = send(lax.dynamic_slice(own, ((1 - core) * half, 0), (half, lanes)), core_route)
    first = place == 0
    start = jnp.concatenate([jnp.where(first, keep, got), jnp.where(first, got, keep)], 1)

    facts = [a.reshape(a.shape[2:]).astype(jnp.float32) for a in (occupancy, up_index, down_index)]
    info = jnp.concatenate(facts, 1)
    other_info = send(info, core_route)
    info = jnp.concatenate([jnp.where(first, info, other_info), jnp.where(first, other_info, info)], 0)

    ham = 0.5 * (hamiltonian + hamiltonian.T)
    mine = lax.dynamic_slice(ham, (core * half, 0), (half, size))
    near = jnp.where(core == 0, mine[:, :half], mine[:, half:])
    far = jnp.where(core == 0, mine[:, half:], mine[:, :half])
    right = jnp.tile(ham, (2 * slots, 2 * slots)) * np.kron(
        np.eye(2 * slots, dtype=np.float32), np.ones((size, size), np.float32)
    )

    flip = (1 - 2 * turn).astype(jnp.float32)
    rows_c = lax.dynamic_slice(couplings, (0, core * half), (couplings.shape[0], half))
    one = jnp.float32(1.0)
    blocks = 4 * slots
    plan = block_plan(2, slots)
    sources = [(0.0, one, one)]
    for p in (0, 1):
        ahead = (mode % 2 == p).astype(jnp.float32)
        sources.append((2.0, ahead, 1.0 - ahead))
    row_w, col_w, damp = [], [], None
    for base, up, down in sources:
        a, b, level = weights_of(plan, info, base, 1.0, up, down, flip, strength, slots)
        row_w.append(a)
        col_w.append(b)
        if damp is None:
            damp = jnp.sum(level * rates[None, :], 1, keepdims=True) * plan[:, 5:6]
    row_part = jnp.dot(jnp.concatenate(row_w, 0), rows_c, precision=HIGHEST)
    row_part = jnp.concatenate([row_part[: damp.shape[0]] - damp, row_part[damp.shape[0] :]], 0)
    column_part = jnp.dot(jnp.concatenate(col_w, 0), couplings, precision=HIGHEST)
    tables = table_of(row_part, column_part, blocks, size).reshape(3, blocks, half, 2 * lanes)
    tables = [tables[0], tables[1], tables[2]]

    edge_plan = block_plan(1, slots)
    links = [p for p in (0, 1) if flat_routes[p]]
    edges = tuple(1 - p for p in links)
    edge_tables = []
    for p in links:
        lower = (chip % 2 == p) & (chip + 1 < tiers // 2)
        upper = (chip % 2 != p) & (chip >= 1)
        up, down = lower.astype(jnp.float32), upper.astype(jnp.float32)
        where = (1 - p) * slots
        pair = []
        for base in (1.0, 3.0):
            a, b, _ = weights_of(edge_plan, info[where : where + slots], base, 0.0, up, down, flip, strength, slots)
            row_part = jnp.dot(a, rows_c, precision=HIGHEST)
            column_part = jnp.dot(b, couplings, precision=HIGHEST)
            pair.append(table_of(row_part, column_part, blocks // 2, size))
        edge_tables.append(pair)

    full = jax.ShapeDtypeStruct((half, 2 * lanes), jnp.float32)
    edge = jax.ShapeDtypeStruct((half, lanes), jnp.float32)
    w = start
    brink = [start[:, q * lanes : (q + 1) * lanes] for q in edges]
    for stage in (4, 3, 2, 1):
        step = TIME_STEP / stage
        flat = [send(brink[n], flat_routes[p]) for n, p in enumerate(links)]
        slant = [send(brink[n], slant_routes[p]) for n, p in enumerate(links)]
        z = send(w, mode_routes[1])
        x = send(w, mode_routes[0])
        other = send(w, core_route)
        part = pl.pallas_call(
            functools.partial(own_kernel, step, size),
            out_shape=full,
            in_specs=[VMEM] * 7,
            out_specs=VMEM,
            scratch_shapes=[pltpu.VMEM((half, 2 * lanes), jnp.float32)],
            name="own_part",
        )(w, other, start, near, far, right, tables[0])
        extra = [a for n in range(len(links)) for a in (flat[n], slant[n], *edge_tables[n])]
        count = len(links) if stage > 1 else 0
        result = pl.pallas_call(
            functools.partial(link_kernel, step, size, edges),
            out_shape=[full] + [edge] * count,
            in_specs=[VMEM] * (5 + len(extra)),
            out_specs=[VMEM] * (1 + count),
            name="link_part",
        )(part, x, z, tables[1], tables[2], *extra)
        w, brink = result[0], result[1:]

    low, high = w[:, :lanes], w[:, lanes:]
    keep = jnp.where(first, low, high)
    got = send(jnp.where(first, high, low), core_route)
    whole = jnp.concatenate([jnp.where(core == 0, keep, got), jnp.where(core == 0, got, keep)], 0)
    return whole.reshape(size, slots * 2, size).transpose(1, 0, 2).reshape(ados.shape)


def solution(mesh):
    spread = P("tier", "mode", None, None)
    in_specs = (P("tier", "mode", None, None, None), P(), P(), P(), P(), spread, spread, spread)
    body = functools.partial(shards, mesh.shape["tier"], mesh.shape["mode"])
    return jax.shard_map(
        body, mesh=mesh, in_specs=in_specs, out_specs=P("tier", "mode", None, None, None), check_vma=False
    )
```

profile of v0, /device:TPU:0, one launch (start us, length us, event | category | flops | bytes accessed | tf_op | source)
XLA Modules:
  0.0 87.0 jit_solution(9965933214980383931)
XLA Ops:
  0.0 0.8 convert_bitcast_fusion.2
  0.8 0.7 convert_bitcast_fusion
  2.0 1.1 %reshape.42 = f32[4,96,96]{2,1,0:T(8,128)S(1)} reshape(f32[1,1,2,2,9216]{4,3,2,1,0:T(2,128)} %param.48) | data formatting | bytes 294912 | tf_op jit(solution)/shard_map/reshape | solution.py:163
  4.1 1.2 %reshape.50.right_ref = f32[384,384]{1,0:T(8,128)} reshape(f32[4,96,4,96]{3,2,1,0:T(4,128)S(1)} %broadcast_multiply_fusion) | data formatting | bytes 1179648 | tf_op jit(solution)/shard_map/mul | solution.py:178
  5.3 0.7 dynamic-slice_select_fusion.2
  8.0 3.1 %convolution_add_fusion = f32[24,48,768]{2,1,0:T(8,128)S(1)} fusion(f32[8,768,1]{1,0,2:T(8,128)S(1)} %copy-done.26, f32[24,768]{1,0:T(8,128)S(1)} %add.82, f32[192,48]{1,0:T(8,128)S(1)} %copy.55), kind=kOutput, calls=%fused_computation | convolution fusion | flops 85819392 | bytes 3674112 | tf_op jit(solution)/shard_map/gea,el->gal/dot_general | solution.py:75
  11.2 1.9 %fusion.75 = (f32[8,48,768]{2,1,0:T(8,128)}, f32[8,48,768]{2,1,0:T(8,128)}, f32[8,48,768]{2,1,0:T(8,128)}) fusion(f32[24,48,768]{2,1,0:T(8,128)S(1)} %convolution_add_fusion), kind=kLoop, calls=%fused_computation.127 | loop fusion | bytes 7077888 | tf_op jit(solution)/shard_map/slice | solution.py:202
  13.9 1.3 %convolution_add_fusion.1.refs_8_ = f32[4,48,384]{2,1,0:T(8,128)} fusion(f32[4,4,48]{2,1,0:T(4,128)S(1)} %bitcast.53, f32[4,384,1]{1,0,2:T(4,128)S(1)} %copy-done.27, f32[4,384]{1,0:T(4,128)S(1)} %add.91), kind=kOutput, calls=%fused_computation.1 | convolution fusion | flops 3612672 | bytes 310272 | tf_op jit(solution)/shard_map/gea,el->gal/dot_general | solution.py:75
  16.0 2.6 %collective-permute-start.3 = (f32[48,768]{1,0:T(8,128)S(1)}, f32[48,768]{1,0:T(8,128)S(1)}, u32[]{:S(2)}, u32[]{:S(2)}) collective-permute-start(f32[48,768]{1,0:T(8,128)S(1)} %pad_maximum_fusion.w_ref.start_ref), channel_id=1, source_target_pairs={{0,1},{1,0},{2,3},{3,2},{4,5},{5,4},{6,7},{7,6},{8,9},{9,8},{10,11... | collective-permute-start | bytes 442376 | tf_op jit(solution)/shard_map/ppermute | solution.py:161
  18.6 3.6 %collective-permute-start.4 = (f32[48,768]{1,0:T(8,128)S(1)}, f32[48,768]{1,0:T(8,128)S(1)}, u32[]{:S(2)}, u32[]{:S(2)}) collective-permute-start(f32[48,768]{1,0:T(8,128)S(1)} %pad_maximum_fusion.w_ref.start_ref), channel_id=1, source_target_pairs={{1,2},{2,1},{3,4},{4,3},{5,6},{6,5},{7,0},{0,7},{9,10},{10,9},{11,... | collective-permute-start | bytes 442376 | tf_op jit(solution)/shard_map/ppermute | solution.py:161
  22.2 1.5 %collective-permute-start.5 = (f32[48,384]{1,0:T(8,128)S(1)}, f32[48,384]{1,0:T(8,128)S(1)}, u32[]{:S(2)}, u32[]{:S(2)}) collective-permute-start(f32[48,384]{1,0:T(8,128)S(1)} %get-tuple-element.26), channel_id=1, source_target_pairs={{0,16},{16,0},{1,17},{17,1},{2,18},{18,2},{3,19},{19,3},{4,20},{20... | collective-permute-start | bytes 221192 | tf_op jit(solution)/shard_map/ppermute | solution.py:161
  23.7 1.3 %convolution_add_fusion.2.refs_7_ = f32[4,48,384]{2,1,0:T(8,128)} fusion(f32[4,4,48]{2,1,0:T(4,128)S(1)} %bitcast.52, f32[4,384,1]{1,0,2:T(4,128)S(1)} %copy-done.27, f32[4,384]{1,0:T(4,128)S(1)} %add.87), kind=kOutput, calls=%fused_computation.2 | convolution fusion | flops 3612672 | bytes 310272 | tf_op jit(solution)/shard_map/gea,el->gal/dot_general | solution.py:75
  25.7 3.1 %own_part.4.refs_0_ = f32[48,768]{1,0:T(8,128)} custom-call(f32[48,768]{1,0:T(8,128)} %copy-done.1, f32[48,768]{1,0:T(8,128)} %copy-done.13, f32[48,768]{1,0:T(8,128)} %copy-done.1, f32[48,48]{1,0:T(8,128)} %get-tuple-element.28.near_ref, f32[48,48]{1,0:T(8,128)} %get-tuple-element.27.far_ref, f32[384,384]{1,0:T(8,128)} %reshape.50.right_ref, ...), custom_call_target="tpu_custom_call" | custom-call | tf_op jit(solution)/shard_map/own_part/pallas_call | solution.py:232
  28.8 0.9 %collective-permute-done.6.refs_6_ = f32[48,384]{1,0:T(8,128)S(1)} collective-permute-done((f32[48,384]{1,0:T(8,128)S(1)}, f32[48,384]{1,0:T(8,128)S(1)}, u32[]{:S(2)}, u32[]{:S(2)}) %collective-permute-start.6) | collective-permute-done | bytes 73760 | tf_op jit(solution)/shard_map/ppermute | solution.py:161
  30.5 2.9 %link_part.4 = (f32[48,768]{1,0:T(8,128)}, f32[48,384]{1,0:T(8,128)}) custom-call(f32[48,768]{1,0:T(8,128)} %own_part.4.refs_0_, f32[48,768]{1,0:T(8,128)} %copy-done.5, f32[48,768]{1,0:T(8,128)} %copy-done.7, f32[8,48,768]{2,1,0:T(8,128)} %get-tuple-element.21.refs_3_, f32[8,48,768]{2,1,0:T(8,128)} %get-tuple-element.20.refs_4_, f32[48,384]{1,0:T(8,128)} %copy-done.16, ...), custom_call_target="tpu_custom_call" | custom-call | tf_op jit(solution)/shard_map/link_part/pallas_call | solution.py:242
  33.4 4.3 %collective-permute-start.9 = (f32[48,768]{1,0:T(8,128)}, f32[48,768]{1,0:T(8,128)S(1)}, u32[]{:S(2)}, u32[]{:S(2)}) collective-permute-start(f32[48,768]{1,0:T(8,128)} %get-tuple-element.11.w_ref), channel_id=1, source_target_pairs={{1,2},{2,1},{3,4},{4,3},{5,6},{6,5},{7,0},{0,7},{9,10},{10,9},{11,... | collective-permute-start | bytes 442376 | tf_op jit(solution)/shard_map/ppermute | solution.py:161
  39.1 3.1 %own_part.5.refs_0_ = f32[48,768]{1,0:T(8,128)} custom-call(f32[48,768]{1,0:T(8,128)} %get-tuple-element.11.w_ref, f32[48,768]{1,0:T(8,128)} %copy-done.14, f32[48,768]{1,0:T(8,128)} %copy-done.1, f32[48,48]{1,0:T(8,128)} %get-tuple-element.28.near_ref, f32[48,48]{1,0:T(8,128)} %get-tuple-element.27.far_ref, f32[384,384]{1,0:T(8,128)} %reshape.50.right_ref, ...), custom_call_target="tpu_custom_call" | custom-call | tf_op jit(solution)/shard_map/own_part/pallas_call | solution.py:232
  42.3 4.2 %collective-permute-done.11.refs_6_ = f32[48,384]{1,0:T(8,128)S(1)} collective-permute-done((f32[48,384]{1,0:T(8,128)}, f32[48,384]{1,0:T(8,128)S(1)}, u32[]{:S(2)}, u32[]{:S(2)}) %collective-permute-start.11) | collective-permute-done | bytes 73760 | tf_op jit(solution)/shard_map/ppermute | solution.py:161
  47.9 2.9 %link_part.5 = (f32[48,768]{1,0:T(8,128)}, f32[48,384]{1,0:T(8,128)}) custom-call(f32[48,768]{1,0:T(8,128)} %own_part.5.refs_0_, f32[48,768]{1,0:T(8,128)} %copy-done.8, f32[48,768]{1,0:T(8,128)} %copy-done.10, f32[8,48,768]{2,1,0:T(8,128)} %get-tuple-element.21.refs_3_, f32[8,48,768]{2,1,0:T(8,128)} %get-tuple-element.20.refs_4_, f32[48,384]{1,0:T(8,128)} %copy-done.18, ...), custom_call_target="tpu_custom_call" | custom-call | tf_op jit(solution)/shard_map/link_part/pallas_call | solution.py:242
  50.8 2.5 %collective-permute-start.14 = (f32[48,768]{1,0:T(8,128)}, f32[48,768]{1,0:T(8,128)S(1)}, u32[]{:S(2)}, u32[]{:S(2)}) collective-permute-start(f32[48,768]{1,0:T(8,128)} %get-tuple-element.13.w_ref), channel_id=1, source_target_pairs={{1,2},{2,1},{3,4},{4,3},{5,6},{6,5},{7,0},{0,7},{9,10},{10,9},{11,... | collective-permute-start | bytes 442376 | tf_op jit(solution)/shard_map/ppermute | solution.py:161
  53.3 0.9 %collective-permute-start.15 = (f32[48,384]{1,0:T(8,128)}, f32[48,384]{1,0:T(8,128)S(1)}, u32[]{:S(2)}, u32[]{:S(2)}) collective-permute-start(f32[48,384]{1,0:T(8,128)} %get-tuple-element.14), channel_id=1, source_target_pairs={{0,16},{16,0},{1,17},{17,1},{2,18},{18,2},{3,19},{19,3},{4,20},{20... | collective-permute-start | bytes 221192 | tf_op jit(solution)/shard_map/ppermute | solution.py:161
  55.0 3.1 %own_part.6.refs_0_ = f32[48,768]{1,0:T(8,128)} custom-call(f32[48,768]{1,0:T(8,128)} %get-tuple-element.13.w_ref, f32[48,768]{1,0:T(8,128)} %copy-done.15, f32[48,768]{1,0:T(8,128)} %copy-done.1, f32[48,48]{1,0:T(8,128)} %get-tuple-element.28.near_ref, f32[48,48]{1,0:T(8,128)} %get-tuple-element.27.far_ref, f32[384,384]{1,0:T(8,128)} %reshape.50.right_ref, ...), custom_call_target="tpu_custom_call" | custom-call | tf_op jit(solution)/shard_map/own_part/pallas_call | solution.py:232
  58.1 4.8 %collective-permute-done.16.refs_6_ = f32[48,384]{1,0:T(8,128)S(1)} collective-permute-done((f32[48,384]{1,0:T(8,128)}, f32[48,384]{1,0:T(8,128)S(1)}, u32[]{:S(2)}, u32[]{:S(2)}) %collective-permute-start.16) | collective-permute-done | bytes 73760 | tf_op jit(solution)/shard_map/ppermute | solution.py:161
  64.2 2.9 %link_part.6 = (f32[48,768]{1,0:T(8,128)}, f32[48,384]{1,0:T(8,128)}) custom-call(f32[48,768]{1,0:T(8,128)} %own_part.6.refs_0_, f32[48,768]{1,0:T(8,128)} %copy-done.9, f32[48,768]{1,0:T(8,128)} %copy-done.11, f32[8,48,768]{2,1,0:T(8,128)} %get-tuple-element.21.refs_3_, f32[8,48,768]{2,1,0:T(8,128)} %get-tuple-element.20.refs_4_, f32[48,384]{1,0:T(8,128)} %copy-done.19, ...), custom_call_target="tpu_custom_call" | custom-call | tf_op jit(solution)/shard_map/link_part/pallas_call | solution.py:242
  67.2 2.4 %collective-permute-start.19 = (f32[48,768]{1,0:T(8,128)}, f32[48,768]{1,0:T(8,128)S(1)}, u32[]{:S(2)}, u32[]{:S(2)}) collective-permute-start(f32[48,768]{1,0:T(8,128)} %get-tuple-element.15.w_ref), channel_id=1, source_target_pairs={{1,2},{2,1},{3,4},{4,3},{5,6},{6,5},{7,0},{0,7},{9,10},{10,9},{11,... | collective-permute-start | bytes 442376 | tf_op jit(solution)/shard_map/ppermute | solution.py:161
  71.3 3.1 %own_part.7.refs_0_ = f32[48,768]{1,0:T(8,128)} custom-call(f32[48,768]{1,0:T(8,128)} %get-tuple-element.15.w_ref, f32[48,768]{1,0:T(8,128)} %copy-done.12, f32[48,768]{1,0:T(8,128)} %copy-done.1, f32[48,48]{1,0:T(8,128)} %get-tuple-element.28.near_ref, f32[48,48]{1,0:T(8,128)} %get-tuple-element.27.far_ref, f32[384,384]{1,0:T(8,128)} %reshape.50.right_ref, ...), custom_call_target="tpu_custom_call" | custom-call | tf_op jit(solution)/shard_map/own_part/pallas_call | solution.py:232
  74.5 4.0 %collective-permute-done.21.refs_6_ = f32[48,384]{1,0:T(8,128)S(1)} collective-permute-done((f32[48,384]{1,0:T(8,128)}, f32[48,384]{1,0:T(8,128)S(1)}, u32[]{:S(2)}, u32[]{:S(2)}) %collective-permute-start.21) | collective-permute-done | bytes 73760 | tf_op jit(solution)/shard_map/ppermute | solution.py:161
  79.8 2.9 %link_part.7 = f32[48,768]{1,0:T(8,128)} custom-call(f32[48,768]{1,0:T(8,128)} %own_part.7.refs_0_, f32[48,768]{1,0:T(8,128)} %copy-done.4, f32[48,768]{1,0:T(8,128)} %copy-done.6, f32[8,48,768]{2,1,0:T(8,128)} %get-tuple-element.21.refs_3_, f32[8,48,768]{2,1,0:T(8,128)} %get-tuple-element.20.refs_4_, f32[48,384]{1,0:T(8,128)} %copy-done.22, ...), custom_call_target="tpu_custom_call" | custom-call | tf_op jit(solution)/shard_map/link_part/pallas_call | solution.py:242
  82.7 0.9 %slice_select_fusion = f32[48,384]{1,0:T(8,128)S(1)} fusion(f32[48,768]{1,0:T(8,128)} %link_part.7, pred[]{:T(512)S(6)} %eq.136), kind=kLoop, calls=%fused_computation.10 | loop fusion | flops 18432 | bytes 221185 | tf_op jit(solution)/shard_map/jit(_where)/select_n | solution.py:253
  83.7 1.3 %collective-permute-done.22 = f32[48,384]{1,0:T(8,128)S(1)} collective-permute-done((f32[48,384]{1,0:T(8,128)S(1)}, f32[48,384]{1,0:T(8,128)S(1)}, u32[]{:S(2)}, u32[]{:S(2)}) %collective-permute-start.22) | collective-permute-done | bytes 73760 | tf_op jit(solution)/shard_map/ppermute | solution.py:161
  85.0 0.9 %broadcast_select_fusion.1 = (f32[48,384]{1,0:T(8,128)S(1)}, f32[48,384]{1,0:T(8,128)S(1)}) fusion(f32[48,384]{1,0:T(8,128)S(1)} %collective-permute-done.22, pred[]{:T(512)S(6)} %eq.135, f32[48,768]{1,0:T(8,128)} %link_part.7, pred[]{:T(512)S(6)} %eq.136), kind=kLoop, calls=%fused_computation.18 | loop fusion | flops 55296 | bytes 368642 | tf_op jit(solution)/shard_map/jit(_where)/select_n | solution.py:254
  86.1 0.9 %reshape.48 = f32[1,1,2,2,9216]{4,3,2,1,0:T(2,128)} reshape(f32[4,96,96]{2,1,0:T(8,128)S(1)} %copy.56) | data formatting | bytes 294912 | tf_op jit(solution)/shard_map/reshape | solution.py:255
  (156 shorter events, 14.4 us)
Async XLA Ops:
  0.0 6.8 %copy-start = (f32[16,96]{1,0:T(8,128)S(1)}, f32[16,96]{1,0:T(8,128)}, u32[]{:S(2)}) copy-start(f32[16,96]{1,0:T(8,128)} %param.50) | copy-start | bytes 18436
  0.0 3.7 %copy-start.2 = (f32[4,96,4,96]{3,2,1,0:T(4,128)S(1)}, f32[4,96,4,96]{3,2,1,0:T(4,128)}, u32[]{:S(2)}) copy-start(f32[4,96,4,96]{3,2,1,0:T(4,128)} %constant.151) | copy-start | bytes 1769476
  0.0 3.6 %copy-start.32 = (f32[2,16]{1,0:T(2,128)S(1)}, f32[2,16]{1,0:T(2,128)}, u32[]{:S(2)}) copy-start(f32[2,16]{1,0:T(2,128)} %param.52) | copy-start | bytes 388
  0.0 3.6 %copy-start.3 = (f32[96,96]{1,0:T(8,128)S(1)}, f32[96,96]{1,0:T(8,128)}, u32[]{:S(2)}) copy-start(f32[96,96]{1,0:T(8,128)} %param.49) | copy-start | bytes 110596
  1.5 4.5 %collective-permute-start.2 = (f32[2,48]{1,0:T(2,128)S(1)}, f32[2,48]{1,0:T(2,128)S(1)}, u32[]{:S(2)}, u32[]{:S(2)}) collective-permute-start(f32[2,48]{1,0:T(2,128)S(1)} %pad_maximum_fusion.3), channel_id=1, source_target_pairs={{0,8},{8,0},{1,9},{9,1},{2,10},{10,2},{3,11},{11,3},{4,12},{12,4},... | collective-permute-start | bytes 1160 | tf_op jit(solution)/shard_map/ppermute | solution.py:161
  3.5 12.1 %collective-permute-start = (f32[48,384]{1,0:T(8,128)S(1)}, f32[48,384]{1,0:T(8,128)S(1)}, u32[]{:S(2)}, u32[]{:S(2)}) collective-permute-start(f32[48,384]{1,0:T(8,128)S(1)} %constant_dynamic-slice_fusion), channel_id=1, source_target_pairs={{0,8},{8,0},{1,9},{9,1},{2,10},{10,2},{3,11},{11,3},{4,12},{12,4},... | collective-permute-start | bytes 221192 | tf_op jit(solution)/shard_map/ppermute | solution.py:161
  4.0 3.9 %copy-start.26 = (f32[8,768,1]{1,0,2:T(8,128)S(1)}, f32[8,768,1]{1,0,2:T(8,128)}, u32[]{:S(2)}) copy-start(f32[8,768,1]{1,0,2:T(8,128)} %constant.153) | copy-start | bytes 73732
  15.6 9.4 %copy-start.1 = (f32[48,768]{1,0:T(8,128)}, f32[48,768]{1,0:T(8,128)S(1)}, u32[]{:S(2)}) copy-start(f32[48,768]{1,0:T(8,128)S(1)} %pad_maximum_fusion.w_ref.start_ref) | copy-start | bytes 442372
  15.6 9.4 %collective-permute-start.1 = (f32[48,768]{1,0:T(8,128)S(1)}, f32[48,768]{1,0:T(8,128)S(1)}, u32[]{:S(2)}, u32[]{:S(2)}) collective-permute-start(f32[48,768]{1,0:T(8,128)S(1)} %pad_maximum_fusion.w_ref.start_ref), channel_id=1, source_target_pairs={{0,8},{8,0},{1,9},{9,1},{2,10},{10,2},{3,11},{11,3},{4,12},{12,4},... | collective-permute-start | bytes 442376 | tf_op jit(solution)/shard_map/ppermute | solution.py:161
  16.0 13.7 %collective-permute-start.3 = (f32[48,768]{1,0:T(8,128)S(1)}, f32[48,768]{1,0:T(8,128)S(1)}, u32[]{:S(2)}, u32[]{:S(2)}) collective-permute-start(f32[48,768]{1,0:T(8,128)S(1)} %pad_maximum_fusion.w_ref.start_ref), channel_id=1, source_target_pairs={{0,1},{1,0},{2,3},{3,2},{4,5},{5,4},{6,7},{7,6},{8,9},{9,8},{10,11... | collective-permute-start | bytes 442376 | tf_op jit(solution)/shard_map/ppermute | solution.py:161
  18.6 11.1 %collective-permute-start.4 = (f32[48,768]{1,0:T(8,128)S(1)}, f32[48,768]{1,0:T(8,128)S(1)}, u32[]{:S(2)}, u32[]{:S(2)}) collective-permute-start(f32[48,768]{1,0:T(8,128)S(1)} %pad_maximum_fusion.w_ref.start_ref), channel_id=1, source_target_pairs={{1,2},{2,1},{3,4},{4,3},{5,6},{6,5},{7,0},{0,7},{9,10},{10,9},{11,... | collective-permute-start | bytes 442376 | tf_op jit(solution)/shard_map/ppermute | solution.py:161
  22.2 6.6 %collective-permute-start.5 = (f32[48,384]{1,0:T(8,128)S(1)}, f32[48,384]{1,0:T(8,128)S(1)}, u32[]{:S(2)}, u32[]{:S(2)}) collective-permute-start(f32[48,384]{1,0:T(8,128)S(1)} %get-tuple-element.26), channel_id=1, source_target_pairs={{0,16},{16,0},{1,17},{17,1},{2,18},{18,2},{3,19},{19,3},{4,20},{20... | collective-permute-start | bytes 221192 | tf_op jit(solution)/shard_map/ppermute | solution.py:161
  23.7 6.0 %collective-permute-start.6 = (f32[48,384]{1,0:T(8,128)S(1)}, f32[48,384]{1,0:T(8,128)S(1)}, u32[]{:S(2)}, u32[]{:S(2)}) collective-permute-start(f32[48,384]{1,0:T(8,128)S(1)} %get-tuple-element.26), channel_id=1, source_target_pairs={{0,17},{17,0},{1,18},{18,1},{2,19},{19,2},{3,20},{20,3},{4,21},{21... | collective-permute-start | bytes 221192 | tf_op jit(solution)/shard_map/ppermute | solution.py:161
  33.4 5.0 %collective-permute-start.7 = (f32[48,768]{1,0:T(8,128)}, f32[48,768]{1,0:T(8,128)S(1)}, u32[]{:S(2)}, u32[]{:S(2)}) collective-permute-start(f32[48,768]{1,0:T(8,128)} %get-tuple-element.11.w_ref), channel_id=1, source_target_pairs={{0,8},{8,0},{1,9},{9,1},{2,10},{10,2},{3,11},{11,3},{4,12},{12,4},... | collective-permute-start | bytes 442376 | tf_op jit(solution)/shard_map/ppermute | solution.py:161
  33.4 13.1 %collective-permute-start.8 = (f32[48,768]{1,0:T(8,128)}, f32[48,768]{1,0:T(8,128)S(1)}, u32[]{:S(2)}, u32[]{:S(2)}) collective-permute-start(f32[48,768]{1,0:T(8,128)} %get-tuple-element.11.w_ref), channel_id=1, source_target_pairs={{0,1},{1,0},{2,3},{3,2},{4,5},{5,4},{6,7},{7,6},{8,9},{9,8},{10,11... | collective-permute-start | bytes 442376 | tf_op jit(solution)/shard_map/ppermute | solution.py:161
  33.4 13.1 %collective-permute-start.9 = (f32[48,768]{1,0:T(8,128)}, f32[48,768]{1,0:T(8,128)S(1)}, u32[]{:S(2)}, u32[]{:S(2)}) collective-permute-start(f32[48,768]{1,0:T(8,128)} %get-tuple-element.11.w_ref), channel_id=1, source_target_pairs={{1,2},{2,1},{3,4},{4,3},{5,6},{6,5},{7,0},{0,7},{9,10},{10,9},{11,... | collective-permute-start | bytes 442376 | tf_op jit(solution)/shard_map/ppermute | solution.py:161
  37.7 4.6 %collective-permute-start.10 = (f32[48,384]{1,0:T(8,128)}, f32[48,384]{1,0:T(8,128)S(1)}, u32[]{:S(2)}, u32[]{:S(2)}) collective-permute-start(f32[48,384]{1,0:T(8,128)} %get-tuple-element.12), channel_id=1, source_target_pairs={{0,16},{16,0},{1,17},{17,1},{2,18},{18,2},{3,19},{19,3},{4,20},{20... | collective-permute-start | bytes 221192 | tf_op jit(solution)/shard_map/ppermute | solution.py:161
  38.4 8.1 %collective-permute-start.11 = (f32[48,384]{1,0:T(8,128)}, f32[48,384]{1,0:T(8,128)S(1)}, u32[]{:S(2)}, u32[]{:S(2)}) collective-permute-start(f32[48,384]{1,0:T(8,128)} %get-tuple-element.12), channel_id=1, source_target_pairs={{0,17},{17,0},{1,18},{18,1},{2,19},{19,2},{3,20},{20,3},{4,21},{21... | collective-permute-start | bytes 221192 | tf_op jit(solution)/shard_map/ppermute | solution.py:161
  42.3 4.2 %copy-start.18 = (f32[48,384]{1,0:T(8,128)}, f32[48,384]{1,0:T(8,128)S(1)}, u32[]{:S(2)}) copy-start(f32[48,384]{1,0:T(8,128)S(1)} %collective-permute-done.10.refs_5_) | copy-start | bytes 221188
  50.8 3.5 %collective-permute-start.12 = (f32[48,768]{1,0:T(8,128)}, f32[48,768]{1,0:T(8,128)S(1)}, u32[]{:S(2)}, u32[]{:S(2)}) collective-permute-start(f32[48,768]{1,0:T(8,128)} %get-tuple-element.13.w_ref), channel_id=1, source_target_pairs={{0,8},{8,0},{1,9},{9,1},{2,10},{10,2},{3,11},{11,3},{4,12},{12,4},... | collective-permute-start | bytes 442376 | tf_op jit(solution)/shard_map/ppermute | solution.py:161
  50.8 12.1 %collective-permute-start.13 = (f32[48,768]{1,0:T(8,128)}, f32[48,768]{1,0:T(8,128)S(1)}, u32[]{:S(2)}, u32[]{:S(2)}) collective-permute-start(f32[48,768]{1,0:T(8,128)} %get-tuple-element.13.w_ref), channel_id=1, source_target_pairs={{0,1},{1,0},{2,3},{3,2},{4,5},{5,4},{6,7},{7,6},{8,9},{9,8},{10,11... | collective-permute-start | bytes 442376 | tf_op jit(solution)/shard_map/ppermute | solution.py:161
  50.8 12.1 %collective-permute-start.14 = (f32[48,768]{1,0:T(8,128)}, f32[48,768]{1,0:T(8,128)S(1)}, u32[]{:S(2)}, u32[]{:S(2)}) collective-permute-start(f32[48,768]{1,0:T(8,128)} %get-tuple-element.13.w_ref), channel_id=1, source_target_pairs={{1,2},{2,1},{3,4},{4,3},{5,6},{6,5},{7,0},{0,7},{9,10},{10,9},{11,... | collective-permute-start | bytes 442376 | tf_op jit(solution)/shard_map/ppermute | solution.py:161
  53.3 4.8 %collective-permute-start.15 = (f32[48,384]{1,0:T(8,128)}, f32[48,384]{1,0:T(8,128)S(1)}, u32[]{:S(2)}, u32[]{:S(2)}) collective-permute-start(f32[48,384]{1,0:T(8,128)} %get-tuple-element.14), channel_id=1, source_target_pairs={{0,16},{16,0},{1,17},{17,1},{2,18},{18,2},{3,19},{19,3},{4,20},{20... | collective-permute-start | bytes 221192 | tf_op jit(solution)/shard_map/ppermute | solution.py:161
  54.2 8.6 %collective-permute-start.16 = (f32[48,384]{1,0:T(8,128)}, f32[48,384]{1,0:T(8,128)S(1)}, u32[]{:S(2)}, u32[]{:S(2)}) collective-permute-start(f32[48,384]{1,0:T(8,128)} %get-tuple-element.14), channel_id=1, source_target_pairs={{0,17},{17,0},{1,18},{18,1},{2,19},{19,2},{3,20},{20,3},{4,21},{21... | collective-permute-start | bytes 221192 | tf_op jit(solution)/shard_map/ppermute | solution.py:161
  58.1 4.8 %copy-start.19 = (f32[48,384]{1,0:T(8,128)}, f32[48,384]{1,0:T(8,128)S(1)}, u32[]{:S(2)}) copy-start(f32[48,384]{1,0:T(8,128)S(1)} %collective-permute-done.15.refs_5_) | copy-start | bytes 221188
  67.2 3.5 %collective-permute-start.17 = (f32[48,768]{1,0:T(8,128)}, f32[48,768]{1,0:T(8,128)S(1)}, u32[]{:S(2)}, u32[]{:S(2)}) collective-permute-start(f32[48,768]{1,0:T(8,128)} %get-tuple-element.15.w_ref), channel_id=1, source_target_pairs={{0,8},{8,0},{1,9},{9,1},{2,10},{10,2},{3,11},{11,3},{4,12},{12,4},... | collective-permute-start | bytes 442376 | tf_op jit(solution)/shard_map/ppermute | solution.py:161
  67.2 11.3 %collective-permute-start.18 = (f32[48,768]{1,0:T(8,128)}, f32[48,768]{1,0:T(8,128)S(1)}, u32[]{:S(2)}, u32[]{:S(2)}) collective-permute-start(f32[48,768]{1,0:T(8,128)} %get-tuple-element.15.w_ref), channel_id=1, source_target_pairs={{0,1},{1,0},{2,3},{3,2},{4,5},{5,4},{6,7},{7,6},{8,9},{9,8},{10,11... | collective-permute-start | bytes 442376 | tf_op jit(solution)/shard_map/ppermute | solution.py:161
  67.2 11.3 %collective-permute-start.19 = (f32[48,768]{1,0:T(8,128)}, f32[48,768]{1,0:T(8,128)S(1)}, u32[]{:S(2)}, u32[]{:S(2)}) collective-permute-start(f32[48,768]{1,0:T(8,128)} %get-tuple-element.15.w_ref), channel_id=1, source_target_pairs={{1,2},{2,1},{3,4},{4,3},{5,6},{6,5},{7,0},{0,7},{9,10},{10,9},{11,... | collective-permute-start | bytes 442376 | tf_op jit(solution)/shard_map/ppermute | solution.py:161
  69.5 4.9 %collective-permute-start.20 = (f32[48,384]{1,0:T(8,128)}, f32[48,384]{1,0:T(8,128)S(1)}, u32[]{:S(2)}, u32[]{:S(2)}) collective-permute-start(f32[48,384]{1,0:T(8,128)} %get-tuple-element.16), channel_id=1, source_target_pairs={{0,16},{16,0},{1,17},{17,1},{2,18},{18,2},{3,19},{19,3},{4,20},{20... | collective-permute-start | bytes 221192 | tf_op jit(solution)/shard_map/ppermute | solution.py:161
  70.2 8.2 %collective-permute-start.21 = (f32[48,384]{1,0:T(8,128)}, f32[48,384]{1,0:T(8,128)S(1)}, u32[]{:S(2)}, u32[]{:S(2)}) collective-permute-start(f32[48,384]{1,0:T(8,128)} %get-tuple-element.16), channel_id=1, source_target_pairs={{0,17},{17,0},{1,18},{18,1},{2,19},{19,2},{3,20},{20,3},{4,21},{21... | collective-permute-start | bytes 221192 | tf_op jit(solution)/shard_map/ppermute | solution.py:161
  74.5 4.0 %copy-start.22 = (f32[48,384]{1,0:T(8,128)}, f32[48,384]{1,0:T(8,128)S(1)}, u32[]{:S(2)}) copy-start(f32[48,384]{1,0:T(8,128)S(1)} %collective-permute-done.20.refs_5_) | copy-start | bytes 221188
  83.6 1.3 %collective-permute-start.22 = (f32[48,384]{1,0:T(8,128)S(1)}, f32[48,384]{1,0:T(8,128)S(1)}, u32[]{:S(2)}, u32[]{:S(2)}) collective-permute-start(f32[48,384]{1,0:T(8,128)S(1)} %slice_select_fusion), channel_id=1, source_target_pairs={{0,8},{8,0},{1,9},{9,1},{2,10},{10,2},{3,11},{11,3},{4,12},{12,4},... | collective-permute-start | bytes 221192 | tf_op jit(solution)/shard_map/ppermute | solution.py:161
  (35 other events, 55.3 us)
where the time goes:
time: 87.4 us; the launch traced here: 87 us
  Pallas kernels  24.3 us (28%)
  starting transfers between devices  20.8 us (24%)
  waiting for transfers between devices  15.3 us (18%)
  local copies, waits for them, and re-layouts  13.6 us (16%)
  matrix products  7.81 us (9%)
  other arithmetic  4.65 us (5%)
    ppermute x23, starting transfers between devices, send(): return lax.ppermute(value, AXES, route)  20.8 us
    ppermute x23, waiting for transfers between devices, send(): return lax.ppermute(value, AXES, route)  15.3 us
    pallas_call x4, Pallas kernels, shards(): pl.pallas_call(functools.partial(own_kernel, step, size), out_shape=full,...  12.6 us
    pallas_call x4, Pallas kernels, shards(): pl.pallas_call(functools.partial(link_kernel, step, size, edges), out_sha...  11.7 us
    unnamed x89, local copies, waits for them, and re-layouts  7.59 us
    dot_general x3, matrix products, table_of(): wide = jnp.einsum('gea,el->gal', rows, spread, precision=HIGHEST)  5.66 us
    slice x1, local copies, waits for them, and re-layouts, shards(): tables = [tables[0], tables[1], tables[2]]  1.89 us
  transfers between devices with their start and end apart: 23, of which 6 were waited for; matrix products, arithmetic and copies ran while one was open for 16% of the time, Pallas kernels for 14%

commit v1 on v0

--- a/solution.py
+++ b/solution.py
@@ -146,6 +146,7 @@
 
 
 VMEM = pl.BlockSpec(memory_space=pltpu.VMEM)
+GRANT = pltpu.CompilerParams(vmem_limit_bytes=16 * 1024 * 1024)
 
 
 def shards(tiers, modes, ados, hamiltonian, couplings, rates, strength, occupancy, up_index, down_index):
@@ -170,6 +171,7 @@
     info = jnp.concatenate(facts, 1)
     other_info = send(info, core_route)
     info = jnp.concatenate([jnp.where(first, info, other_info), jnp.where(first, other_info, info)], 0)
+    start, info = lax.optimization_barrier((start, info))
 
     ham = 0.5 * (hamiltonian + hamiltonian.T)
     mine = lax.dynamic_slice(ham, (core * half, 0), (half, size))
@@ -235,6 +237,7 @@
             in_specs=[VMEM] * 7,
             out_specs=VMEM,
             scratch_shapes=[pltpu.VMEM((half, 2 * lanes), jnp.float32)],
+            compiler_params=GRANT,
             name="own_part",
         )(w, other, start, near, far, right, tables[0])
         extra = [a for n in range(len(links)) for a in (flat[n], slant[n], *edge_tables[n])]
@@ -244,6 +247,7 @@
             out_shape=[full] + [edge] * count,
             in_specs=[VMEM] * (5 + len(extra)),
             out_specs=[VMEM] * (1 + count),
+            compiler_params=GRANT,
             name="link_part",
         )(part, x, z, tables[1], tables[2], *extra)
         w, brink = result[0], result[1:]

time: 87.4 us -> 75.3 us (0.86)
  Pallas kernels: 24.3 us -> 9.41 us
  waiting for transfers between devices: 15.3 us -> 19.1 us
  local copies, waits for them, and re-layouts: 13.6 us -> 9.89 us
  starting transfers between devices: 20.8 us -> 22.6 us
  matrix products: 7.81 us -> 9.35 us
  other arithmetic: 4.65 us -> 3.57 us
    pallas_call x4, Pallas kernels: 11.7 us -> 2.33 us  [shards(): pl.pallas_call(functools.partial(link_kernel, step, size, edges), out_sha...]
    pallas_call x4, Pallas kernels: 12.6 us -> 7.08 us  [shards(): pl.pallas_call(functools.partial(own_kernel, step, size), out_shape=full,...]
    unnamed x89 -> x55, local copies, waits for them, and re-layouts: 7.59 us -> 2.75 us
    ppermute x23, waiting for transfers between devices: 15.3 us -> 19.1 us  [send(): return lax.ppermute(value, AXES, route)]
    ppermute x23, starting transfers between devices: 20.8 us -> 22.6 us  [send(): return lax.ppermute(value, AXES, route)]
    slice x1, local copies, waits for them, and re-layouts: 1.89 us -> 0.23 us  [shards(): tables = [tables[0], tables[1], tables[2]]]
    slice x0 -> x1, local copies, waits for them, and re-layouts: none -> 1.54 us  [shards(): brink = [start[:, q * lanes:(q + 1) * lanes] for q in edges]]
    add x3, local copies, waits for them, and re-layouts: 0.26 us -> 1.52 us  [table_of(): return wide + column_part.reshape(groups, 1, blocks * width)]
  transfers between devices with their start and end apart: 23 -> 23, of which waited for: 6 -> 7; matrix products, arithmetic and copies ran while one was open for 16% -> 19% of each run, Pallas kernels for 14% -> 9%
where the time goes in v1:
time: 75.3 us; the launch traced here: 74.7 us
  starting transfers between devices  22.6 us (30%)
  waiting for transfers between devices  19.1 us (25%)
  local copies, waits for them, and re-layouts  9.89 us (13%)
  Pallas kernels  9.41 us (12%)
  matrix products  9.35 us (12%)
  other arithmetic  3.57 us (5%)
    ppermute x23, starting transfers between devices, send(): return lax.ppermute(value, AXES, route)  22.6 us
    ppermute x23, waiting for transfers between devices, send(): return lax.ppermute(value, AXES, route)  19.1 us
    pallas_call x4, Pallas kernels, shards(): pl.pallas_call(functools.partial(own_kernel, step, size), out_shape=full,...  7.08 us
    dot_general x3, matrix products, table_of(): wide = jnp.einsum('gea,el->gal', rows, spread, precision=HIGHEST)  5.64 us
    unnamed x55, local copies, waits for them, and re-layouts  2.75 us
    pallas_call x4, Pallas kernels, shards(): pl.pallas_call(functools.partial(link_kernel, step, size, edges), out_sha...  2.33 us
    dot_general x2, matrix products, shards(): row_part = jnp.dot(a, rows_c, precision=HIGHEST)  1.62 us
    slice x1, local copies, waits for them, and re-layouts, shards(): brink = [start[:, q * lanes:(q + 1) * lanes] for q in edges]  1.54 us
  transfers between devices with their start and end apart: 23, of which 7 were waited for; matrix products, arithmetic and copies ran while one was open for 19% of the time, Pallas kernels for 9%

profile of v1, /device:TPU:0, one launch (start us, length us, event | category | flops | bytes accessed | tf_op | source)
XLA Modules:
  0.0 74.7 jit_solution(7135011719617526081)
XLA Ops:
  2.0 1.1 %reshape.42 = f32[4,96,96]{2,1,0:T(8,128)S(1)} reshape(f32[1,1,2,2,9216]{4,3,2,1,0:T(2,128)} %param.48) | data formatting | bytes 294912 | tf_op jit(solution)/shard_map/reshape | solution.py:164
  4.0 1.2 %reshape.50.right_ref = f32[384,384]{1,0:T(8,128)} reshape(f32[4,96,4,96]{3,2,1,0:T(4,128)S(1)} %broadcast_multiply_fusion) | data formatting | bytes 1179648 | tf_op jit(solution)/shard_map/mul | solution.py:180
  7.1 0.8 %fusion.17 = f32[16,48]{1,0:T(8,128)} fusion(f32[16,96]{1,0:T(8,128)S(1)} %copy-done, s32[]{:T(128)S(6)} %select_n.124, f32[16,48]{1,0:T(8,128)S(1)} %fusion.57, f32[]{:T(128)S(6)} %select.21, f32[16]{0:T(128)S(1)} %copy-done.26, f32[16]{0:T(128)S(1)} %get-tuple-element.48, f32[16]{0:T(128)S(1)} %copy-done.25, f32[16]{0:T(128)S(1)} %get-tuple-element.47, ...), kind=kOutput, calls=%fused_computation.35 | convolution fusion | flops 150016 | bytes 38412 | tf_op jit(solution)/shard_map/dot_general | solution.py:218
  8.1 0.8 %fusion.23 = f32[16,48]{1,0:T(8,128)} fusion(f32[16,96]{1,0:T(8,128)S(1)} %copy-done, s32[]{:T(128)S(6)} %select_n.124, f32[16,48]{1,0:T(8,128)S(1)} %fusion.57, f32[]{:T(128)S(6)} %select.21, f32[16]{0:T(128)S(1)} %get-tuple-element.48, f32[16]{0:T(128)S(1)} %copy-done.25, f32[16]{0:T(128)S(1)} %get-tuple-element.47, f32[16]{0:T(128)S(1)} %copy-done.24, ...), kind=kOutput, calls=%fused_computation.43 | convolution fusion | flops 150016 | bytes 38412 | tf_op jit(solution)/shard_map/dot_general | solution.py:218
  8.9 0.8 %fusion.20 = f32[16,96]{1,0:T(8,128)} fusion(f32[16,96]{1,0:T(8,128)S(1)} %copy-done, f32[16,48]{1,0:T(8,128)S(1)} %fusion.57, f32[]{:T(128)S(6)} %select.21, f32[16]{0:T(128)S(1)} %copy-done.23, f32[16]{0:T(128)S(1)} %get-tuple-element.48, f32[16]{0:T(128)S(1)} %get-tuple-element.47, f32[16]{0:T(128)S(1)} %copy-done.24, pred[16]{0:T(512)(128)(4,1)S(1)} %copy-done.22, ...), kind=kOutput, calls=%fused_computation.40 | convolution fusion | flops 297472 | bytes 41480 | tf_op jit(solution)/shard_map/dot_general | solution.py:219
  10.1 2.6 %collective-permute-start.3 = (f32[48,768]{1,0:T(8,128)}, f32[48,768]{1,0:T(8,128)}, u32[]{:S(2)}, u32[]{:S(2)}) collective-permute-start(f32[48,768]{1,0:T(8,128)} %pad_maximum_fusion.w_ref.start_ref), channel_id=1, source_target_pairs={{0,1},{1,0},{2,3},{3,2},{4,5},{5,4},{6,7},{7,6},{8,9},{9,8},{10,11... | collective-permute-start | bytes 442376 | tf_op jit(solution)/shard_map/ppermute | solution.py:162
  12.7 3.6 %collective-permute-start.4 = (f32[48,768]{1,0:T(8,128)}, f32[48,768]{1,0:T(8,128)}, u32[]{:S(2)}, u32[]{:S(2)}) collective-permute-start(f32[48,768]{1,0:T(8,128)} %pad_maximum_fusion.w_ref.start_ref), channel_id=1, source_target_pairs={{1,2},{2,1},{3,4},{4,3},{5,6},{6,5},{7,0},{0,7},{9,10},{10,9},{11,... | collective-permute-start | bytes 442376 | tf_op jit(solution)/shard_map/ppermute | solution.py:162
  16.2 1.5 %slice.116 = f32[48,384]{1,0:T(8,128)} slice(f32[48,768]{1,0:T(8,128)} %pad_maximum_fusion.w_ref.start_ref), slice={[0:48], [384:768]} | slice | bytes 147456 | tf_op jit(solution)/shard_map/slice | solution.py:226
  17.8 1.5 %collective-permute-start.5 = (f32[48,384]{1,0:T(8,128)}, f32[48,384]{1,0:T(8,128)}, u32[]{:S(2)}, u32[]{:S(2)}) collective-permute-start(f32[48,384]{1,0:T(8,128)} %slice.116), channel_id=1, source_target_pairs={{0,16},{16,0},{1,17},{17,1},{2,18},{18,2},{3,19},{19,3},{4,20},{20... | collective-permute-start | bytes 221192 | tf_op jit(solution)/shard_map/ppermute | solution.py:162
  21.0 3.1 %convolution_add_fusion = f32[24,48,768]{2,1,0:T(8,128)S(1)} fusion(f32[8,768,1]{1,0,2:T(8,128)S(1)} %copy-done.10, f32[24,768]{1,0:T(8,128)S(1)} %add.82, f32[192,48]{1,0:T(8,128)S(1)} %copy.55), kind=kOutput, calls=%fused_computation | convolution fusion | flops 85819392 | bytes 3674112 | tf_op jit(solution)/shard_map/gea,el->gal/dot_general | solution.py:75
  25.8 1.3 %convolution_add_fusion.1.refs_8_ = f32[4,48,384]{2,1,0:T(8,128)S(1)} fusion(f32[4,4,48]{2,1,0:T(4,128)} %bitcast.51, f32[4,384,1]{1,0,2:T(4,128)} %constant.152, f32[4,384]{1,0:T(4,128)} %add.91), kind=kOutput, calls=%fused_computation.1 | convolution fusion | flops 3612672 | bytes 310272 | tf_op jit(solution)/shard_map/gea,el->gal/dot_general | solution.py:75
  27.0 1.3 %convolution_add_fusion.2.refs_7_ = f32[4,48,384]{2,1,0:T(8,128)S(1)} fusion(f32[4,4,48]{2,1,0:T(4,128)} %bitcast.50, f32[4,384,1]{1,0,2:T(4,128)} %constant.152, f32[4,384]{1,0:T(4,128)S(1)} %add.87), kind=kOutput, calls=%fused_computation.2 | convolution fusion | flops 3612672 | bytes 310272 | tf_op jit(solution)/shard_map/gea,el->gal/dot_general | solution.py:75
  28.3 1.1 %copy-done.1 = f32[384,384]{1,0:T(8,128)S(1)} copy-done((f32[384,384]{1,0:T(8,128)S(1)}, f32[384,384]{1,0:T(8,128)}, u32[]{:S(2)}) %copy-start.1) | copy-done | bytes 589848
  30.9 1.9 %own_part.4.refs_0_ = f32[48,768]{1,0:T(8,128)S(1)} custom-call(f32[48,768]{1,0:T(8,128)} %pad_maximum_fusion.w_ref.start_ref, f32[48,768]{1,0:T(8,128)} %collective-permute-done.2.other_ref, f32[48,768]{1,0:T(8,128)} %pad_maximum_fusion.w_ref.start_ref, f32[48,48]{1,0:T(8,128)S(1)} %copy-done.5, f32[48,48]{1,0:T(8,128)S(1)} %copy-done.3, ...), custom_call_target="tpu_custom_call" | custom-call | tf_op jit(solution)/shard_map/own_part/pallas_call | solution.py:234
  32.8 1.4 %link_part.4 = (f32[48,768]{1,0:T(8,128)S(1)}, f32[48,384]{1,0:T(8,128)S(1)}) custom-call(f32[48,768]{1,0:T(8,128)S(1)} %own_part.4.refs_0_, f32[48,768]{1,0:T(8,128)} %collective-permute-done.3.refs_1_, f32[48,768]{1,0:T(8,128)} %collective-permute-done.4.refs_2_, f32[8,48,768]{2,1,0:T(8,128)S(1)} %get-tuple-element.25.refs_3_, ...), custom_call_target="tpu_custom_call" | custom-call | tf_op jit(solution)/shard_map/link_part/pallas_call | solution.py:245
  34.4 4.7 %collective-permute-start.9 = (f32[48,768]{1,0:T(8,128)S(1)}, f32[48,768]{1,0:T(8,128)S(1)}, u32[]{:S(2)}, u32[]{:S(2)}) collective-permute-start(f32[48,768]{1,0:T(8,128)S(1)} %get-tuple-element.15.w_ref), channel_id=1, source_target_pairs={{1,2},{2,1},{3,4},{4,3},{5,6},{6,5},{7,0},{0,7},{9,10},{10,9},{11,... | collective-permute-start | bytes 442376 | tf_op jit(solution)/shard_map/ppermute | solution.py:162
  39.1 1.1 %collective-permute-start.10 = (f32[48,384]{1,0:T(8,128)S(1)}, f32[48,384]{1,0:T(8,128)S(1)}, u32[]{:S(2)}, u32[]{:S(2)}) collective-permute-start(f32[48,384]{1,0:T(8,128)S(1)} %get-tuple-element.16), channel_id=1, source_target_pairs={{0,16},{16,0},{1,17},{17,1},{2,18},{18,2},{3,19},{19,3},{4,20},{20... | collective-permute-start | bytes 221192 | tf_op jit(solution)/shard_map/ppermute | solution.py:162
  40.3 1.7 %own_part.5.refs_0_ = f32[48,768]{1,0:T(8,128)S(1)} custom-call(f32[48,768]{1,0:T(8,128)S(1)} %get-tuple-element.15.w_ref, f32[48,768]{1,0:T(8,128)S(1)} %collective-permute-done.7.other_ref, f32[48,768]{1,0:T(8,128)} %pad_maximum_fusion.w_ref.start_ref, f32[48,48]{1,0:T(8,128)S(1)} %copy-done.6, f32[48,48]{1,0:T(8,128)S(1)} %copy-done.4, ...), custom_call_target="tpu_custom_call" | custom-call | tf_op jit(solution)/shard_map/own_part/pallas_call | solution.py:234
  42.0 1.5 %collective-permute-done.10.refs_5_ = f32[48,384]{1,0:T(8,128)S(1)} collective-permute-done((f32[48,384]{1,0:T(8,128)S(1)}, f32[48,384]{1,0:T(8,128)S(1)}, u32[]{:S(2)}, u32[]{:S(2)}) %collective-permute-start.10) | collective-permute-done | bytes 73760 | tf_op jit(solution)/shard_map/ppermute | solution.py:162
  43.5 4.0 %collective-permute-done.11.refs_6_ = f32[48,384]{1,0:T(8,128)S(1)} collective-permute-done((f32[48,384]{1,0:T(8,128)S(1)}, f32[48,384]{1,0:T(8,128)S(1)}, u32[]{:S(2)}, u32[]{:S(2)}) %collective-permute-start.11) | collective-permute-done | bytes 73760 | tf_op jit(solution)/shard_map/ppermute | solution.py:162
  48.0 3.1 %collective-permute-start.14 = (f32[48,768]{1,0:T(8,128)S(1)}, f32[48,768]{1,0:T(8,128)S(1)}, u32[]{:S(2)}, u32[]{:S(2)}) collective-permute-start(f32[48,768]{1,0:T(8,128)S(1)} %get-tuple-element.17.w_ref), channel_id=1, source_target_pairs={{1,2},{2,1},{3,4},{4,3},{5,6},{6,5},{7,0},{0,7},{9,10},{10,9},{11,... | collective-permute-start | bytes 442376 | tf_op jit(solution)/shard_map/ppermute | solution.py:162
  51.1 0.9 %collective-permute-start.15 = (f32[48,384]{1,0:T(8,128)S(1)}, f32[48,384]{1,0:T(8,128)S(1)}, u32[]{:S(2)}, u32[]{:S(2)}) collective-permute-start(f32[48,384]{1,0:T(8,128)S(1)} %get-tuple-element.18), channel_id=1, source_target_pairs={{0,16},{16,0},{1,17},{17,1},{2,18},{18,2},{3,19},{19,3},{4,20},{20... | collective-permute-start | bytes 221192 | tf_op jit(solution)/shard_map/ppermute | solution.py:162
  52.0 1.7 %own_part.6.refs_0_ = f32[48,768]{1,0:T(8,128)S(1)} custom-call(f32[48,768]{1,0:T(8,128)S(1)} %get-tuple-element.17.w_ref, f32[48,768]{1,0:T(8,128)S(1)} %collective-permute-done.12.other_ref, f32[48,768]{1,0:T(8,128)} %pad_maximum_fusion.w_ref.start_ref, f32[48,48]{1,0:T(8,128)S(1)} %copy-done.6, f32[48,48]{1,0:T(8,128)S(1)} %copy-done.4, ...), custom_call_target="tpu_custom_call" | custom-call | tf_op jit(solution)/shard_map/own_part/pallas_call | solution.py:234
  53.7 1.7 %collective-permute-done.15.refs_5_ = f32[48,384]{1,0:T(8,128)S(1)} collective-permute-done((f32[48,384]{1,0:T(8,128)S(1)}, f32[48,384]{1,0:T(8,128)S(1)}, u32[]{:S(2)}, u32[]{:S(2)}) %collective-permute-start.15) | collective-permute-done | bytes 73760 | tf_op jit(solution)/shard_map/ppermute | solution.py:162
  55.4 4.5 %collective-permute-done.16.refs_6_ = f32[48,384]{1,0:T(8,128)S(1)} collective-permute-done((f32[48,384]{1,0:T(8,128)S(1)}, f32[48,384]{1,0:T(8,128)S(1)}, u32[]{:S(2)}, u32[]{:S(2)}) %collective-permute-start.16) | collective-permute-done | bytes 73760 | tf_op jit(solution)/shard_map/ppermute | solution.py:162
  60.4 2.6 %collective-permute-start.19 = (f32[48,768]{1,0:T(8,128)S(1)}, f32[48,768]{1,0:T(8,128)S(1)}, u32[]{:S(2)}, u32[]{:S(2)}) collective-permute-start(f32[48,768]{1,0:T(8,128)S(1)} %get-tuple-element.19.w_ref), channel_id=1, source_target_pairs={{1,2},{2,1},{3,4},{4,3},{5,6},{6,5},{7,0},{0,7},{9,10},{10,9},{11,... | collective-permute-start | bytes 442376 | tf_op jit(solution)/shard_map/ppermute | solution.py:162
  63.0 0.9 %collective-permute-start.20 = (f32[48,384]{1,0:T(8,128)S(1)}, f32[48,384]{1,0:T(8,128)S(1)}, u32[]{:S(2)}, u32[]{:S(2)}) collective-permute-start(f32[48,384]{1,0:T(8,128)S(1)} %get-tuple-element.20), channel_id=1, source_target_pairs={{0,16},{16,0},{1,17},{17,1},{2,18},{18,2},{3,19},{19,3},{4,20},{20... | collective-permute-start | bytes 221192 | tf_op jit(solution)/shard_map/ppermute | solution.py:162
  63.9 1.7 %own_part.7.refs_0_ = f32[48,768]{1,0:T(8,128)S(1)} custom-call(f32[48,768]{1,0:T(8,128)S(1)} %get-tuple-element.19.w_ref, f32[48,768]{1,0:T(8,128)S(1)} %collective-permute-done.17.other_ref, f32[48,768]{1,0:T(8,128)} %pad_maximum_fusion.w_ref.start_ref, f32[48,48]{1,0:T(8,128)S(1)} %copy-done.6, f32[48,48]{1,0:T(8,128)S(1)} %copy-done.4, ...), custom_call_target="tpu_custom_call" | custom-call | tf_op jit(solution)/shard_map/own_part/pallas_call | solution.py:234
  65.7 1.7 %collective-permute-done.20.refs_5_ = f32[48,384]{1,0:T(8,128)S(1)} collective-permute-done((f32[48,384]{1,0:T(8,128)S(1)}, f32[48,384]{1,0:T(8,128)S(1)}, u32[]{:S(2)}, u32[]{:S(2)}) %collective-permute-start.20) | collective-permute-done | bytes 73760 | tf_op jit(solution)/shard_map/ppermute | solution.py:162
  67.4 4.5 %collective-permute-done.21.refs_6_ = f32[48,384]{1,0:T(8,128)S(1)} collective-permute-done((f32[48,384]{1,0:T(8,128)S(1)}, f32[48,384]{1,0:T(8,128)S(1)}, u32[]{:S(2)}, u32[]{:S(2)}) %collective-permute-start.21) | collective-permute-done | bytes 73760 | tf_op jit(solution)/shard_map/ppermute | solution.py:162
  72.3 1.3 %collective-permute-done.22 = f32[48,384]{1,0:T(8,128)S(1)} collective-permute-done((f32[48,384]{1,0:T(8,128)S(1)}, f32[48,384]{1,0:T(8,128)S(1)}, u32[]{:S(2)}, u32[]{:S(2)}) %collective-permute-start.22) | collective-permute-done | bytes 73760 | tf_op jit(solution)/shard_map/ppermute | solution.py:162
  73.8 0.9 %reshape.48 = f32[1,1,2,2,9216]{4,3,2,1,0:T(2,128)} reshape(f32[4,96,96]{2,1,0:T(8,128)S(1)} %copy.56) | data formatting | bytes 294912 | tf_op jit(solution)/shard_map/reshape | solution.py:259
  (124 shorter events, 11.4 us)
Async XLA Ops:
  1.5 4.5 %collective-permute-start.1 = (f32[2,48]{1,0:T(2,128)S(1)}, f32[2,48]{1,0:T(2,128)S(1)}, u32[]{:S(2)}, u32[]{:S(2)}) collective-permute-start(f32[2,48]{1,0:T(2,128)S(1)} %pad_maximum_fusion.4), channel_id=1, source_target_pairs={{0,8},{8,0},{1,9},{9,1},{2,10},{10,2},{3,11},{11,3},{4,12},{12,4},... | collective-permute-start | bytes 1160 | tf_op jit(solution)/shard_map/ppermute | solution.py:162
  3.5 2.7 %collective-permute-start = (f32[48,384]{1,0:T(8,128)S(1)}, f32[48,384]{1,0:T(8,128)S(1)}, u32[]{:S(2)}, u32[]{:S(2)}) collective-permute-start(f32[48,384]{1,0:T(8,128)S(1)} %constant_dynamic-slice_fusion), channel_id=1, source_target_pairs={{0,8},{8,0},{1,9},{9,1},{2,10},{10,2},{3,11},{11,3},{4,12},{12,4},... | collective-permute-start | bytes 221192 | tf_op jit(solution)/shard_map/ppermute | solution.py:162
  4.0 15.3 %copy-start.9 = (f32[64,4]{1,0:T(8,128)S(1)}, f32[64,4]{1,0:T(8,128)}, u32[]{:S(2)}) copy-start(f32[64,4]{1,0:T(8,128)} %constant.114.clone) | copy-start | bytes 3076
  5.2 14.3 %copy-start.12 = (pred[64]{0:T(512)(128)(4,1)S(1)}, pred[64]{0:T(512)(128)(4,1)}, u32[]{:S(2)}) copy-start(pred[64]{0:T(512)(128)(4,1)} %constant.139) | copy-start | bytes 196
  5.2 14.3 %copy-start.13 = (f32[64]{0:T(128)S(1)}, f32[64]{0:T(128)}, u32[]{:S(2)}) copy-start(f32[64]{0:T(128)} %constant.141) | copy-start | bytes 772
  5.3 14.3 %copy-start.14 = (f32[64]{0:T(128)S(1)}, f32[64]{0:T(128)}, u32[]{:S(2)}) copy-start(f32[64]{0:T(128)} %constant.143) | copy-start | bytes 772
  5.3 14.3 %copy-start.16 = (f32[64]{0:T(128)S(1)}, f32[64]{0:T(128)}, u32[]{:S(2)}) copy-start(f32[64]{0:T(128)} %constant.140) | copy-start | bytes 772
  5.3 14.4 %copy-start.19 = (f32[16]{0:T(128)S(1)}, f32[16]{0:T(128)}, u32[]{:S(2)}) copy-start(f32[16]{0:T(128)} %param.51) | copy-start | bytes 196
  5.3 14.4 %copy-start.20 = (f32[64]{0:T(128)S(1)}, f32[64]{0:T(128)}, u32[]{:S(2)}) copy-start(f32[64]{0:T(128)} %constant.142) | copy-start | bytes 772
  5.3 15.0 %copy-start.21 = (f32[64]{0:T(128)S(1)}, f32[64]{0:T(128)}, u32[]{:S(2)}) copy-start(f32[64]{0:T(128)} %constant.150) | copy-start | bytes 772
  6.2 14.8 %copy-start.10 = (f32[8,768,1]{1,0,2:T(8,128)S(1)}, f32[8,768,1]{1,0,2:T(8,128)}, u32[]{:S(2)}) copy-start(f32[8,768,1]{1,0,2:T(8,128)} %constant.151) | copy-start | bytes 73732
  9.7 18.6 %collective-permute-start.2 = (f32[48,768]{1,0:T(8,128)}, f32[48,768]{1,0:T(8,128)}, u32[]{:S(2)}, u32[]{:S(2)}) collective-permute-start(f32[48,768]{1,0:T(8,128)} %pad_maximum_fusion.w_ref.start_ref), channel_id=1, source_target_pairs={{0,8},{8,0},{1,9},{9,1},{2,10},{10,2},{3,11},{11,3},{4,12},{12,4},... | collective-permute-start | bytes 442376 | tf_op jit(solution)/shard_map/ppermute | solution.py:162
  10.1 22.7 %collective-permute-start.3 = (f32[48,768]{1,0:T(8,128)}, f32[48,768]{1,0:T(8,128)}, u32[]{:S(2)}, u32[]{:S(2)}) collective-permute-start(f32[48,768]{1,0:T(8,128)} %pad_maximum_fusion.w_ref.start_ref), channel_id=1, source_target_pairs={{0,1},{1,0},{2,3},{3,2},{4,5},{5,4},{6,7},{7,6},{8,9},{9,8},{10,11... | collective-permute-start | bytes 442376 | tf_op jit(solution)/shard_map/ppermute | solution.py:162
  12.7 20.1 %collective-permute-start.4 = (f32[48,768]{1,0:T(8,128)}, f32[48,768]{1,0:T(8,128)}, u32[]{:S(2)}, u32[]{:S(2)}) collective-permute-start(f32[48,768]{1,0:T(8,128)} %pad_maximum_fusion.w_ref.start_ref), channel_id=1, source_target_pairs={{1,2},{2,1},{3,4},{4,3},{5,6},{6,5},{7,0},{0,7},{9,10},{10,9},{11,... | collective-permute-start | bytes 442376 | tf_op jit(solution)/shard_map/ppermute | solution.py:162
  17.8 15.0 %collective-permute-start.5 = (f32[48,384]{1,0:T(8,128)}, f32[48,384]{1,0:T(8,128)}, u32[]{:S(2)}, u32[]{:S(2)}) collective-permute-start(f32[48,384]{1,0:T(8,128)} %slice.116), channel_id=1, source_target_pairs={{0,16},{16,0},{1,17},{17,1},{2,18},{18,2},{3,19},{19,3},{4,20},{20... | collective-permute-start | bytes 221192 | tf_op jit(solution)/shard_map/ppermute | solution.py:162
  19.3 13.4 %collective-permute-start.6 = (f32[48,384]{1,0:T(8,128)}, f32[48,384]{1,0:T(8,128)}, u32[]{:S(2)}, u32[]{:S(2)}) collective-permute-start(f32[48,384]{1,0:T(8,128)} %slice.116), channel_id=1, source_target_pairs={{0,17},{17,0},{1,18},{18,1},{2,19},{19,2},{3,20},{20,3},{4,21},{21... | collective-permute-start | bytes 221192 | tf_op jit(solution)/shard_map/ppermute | solution.py:162
  34.3 6.0 %collective-permute-start.7 = (f32[48,768]{1,0:T(8,128)S(1)}, f32[48,768]{1,0:T(8,128)S(1)}, u32[]{:S(2)}, u32[]{:S(2)}) collective-permute-start(f32[48,768]{1,0:T(8,128)S(1)} %get-tuple-element.15.w_ref), channel_id=1, source_target_pairs={{0,8},{8,0},{1,9},{9,1},{2,10},{10,2},{3,11},{11,3},{4,12},{12,4},... | collective-permute-start | bytes 442376 | tf_op jit(solution)/shard_map/ppermute | solution.py:162
  34.3 13.2 %collective-permute-start.8 = (f32[48,768]{1,0:T(8,128)S(1)}, f32[48,768]{1,0:T(8,128)S(1)}, u32[]{:S(2)}, u32[]{:S(2)}) collective-permute-start(f32[48,768]{1,0:T(8,128)S(1)} %get-tuple-element.15.w_ref), channel_id=1, source_target_pairs={{0,1},{1,0},{2,3},{3,2},{4,5},{5,4},{6,7},{7,6},{8,9},{9,8},{10,11... | collective-permute-start | bytes 442376 | tf_op jit(solution)/shard_map/ppermute | solution.py:162
  34.4 13.1 %collective-permute-start.9 = (f32[48,768]{1,0:T(8,128)S(1)}, f32[48,768]{1,0:T(8,128)S(1)}, u32[]{:S(2)}, u32[]{:S(2)}) collective-permute-start(f32[48,768]{1,0:T(8,128)S(1)} %get-tuple-element.15.w_ref), channel_id=1, source_target_pairs={{1,2},{2,1},{3,4},{4,3},{5,6},{6,5},{7,0},{0,7},{9,10},{10,9},{11,... | collective-permute-start | bytes 442376 | tf_op jit(solution)/shard_map/ppermute | solution.py:162
  39.1 4.4 %collective-permute-start.10 = (f32[48,384]{1,0:T(8,128)S(1)}, f32[48,384]{1,0:T(8,128)S(1)}, u32[]{:S(2)}, u32[]{:S(2)}) collective-permute-start(f32[48,384]{1,0:T(8,128)S(1)} %get-tuple-element.16), channel_id=1, source_target_pairs={{0,16},{16,0},{1,17},{17,1},{2,18},{18,2},{3,19},{19,3},{4,20},{20... | collective-permute-start | bytes 221192 | tf_op jit(solution)/shard_map/ppermute | solution.py:162
  40.3 7.2 %collective-permute-start.11 = (f32[48,384]{1,0:T(8,128)S(1)}, f32[48,384]{1,0:T(8,128)S(1)}, u32[]{:S(2)}, u32[]{:S(2)}) collective-permute-start(f32[48,384]{1,0:T(8,128)S(1)} %get-tuple-element.16), channel_id=1, source_target_pairs={{0,17},{17,0},{1,18},{18,1},{2,19},{19,2},{3,20},{20,3},{4,21},{21... | collective-permute-start | bytes 221192 | tf_op jit(solution)/shard_map/ppermute | solution.py:162
  47.8 4.2 %collective-permute-start.12 = (f32[48,768]{1,0:T(8,128)S(1)}, f32[48,768]{1,0:T(8,128)S(1)}, u32[]{:S(2)}, u32[]{:S(2)}) collective-permute-start(f32[48,768]{1,0:T(8,128)S(1)} %get-tuple-element.17.w_ref), channel_id=1, source_target_pairs={{0,8},{8,0},{1,9},{9,1},{2,10},{10,2},{3,11},{11,3},{4,12},{12,4},... | collective-permute-start | bytes 442376 | tf_op jit(solution)/shard_map/ppermute | solution.py:162
  47.9 12.0 %collective-permute-start.13 = (f32[48,768]{1,0:T(8,128)S(1)}, f32[48,768]{1,0:T(8,128)S(1)}, u32[]{:S(2)}, u32[]{:S(2)}) collective-permute-start(f32[48,768]{1,0:T(8,128)S(1)} %get-tuple-element.17.w_ref), channel_id=1, source_target_pairs={{0,1},{1,0},{2,3},{3,2},{4,5},{5,4},{6,7},{7,6},{8,9},{9,8},{10,11... | collective-permute-start | bytes 442376 | tf_op jit(solution)/shard_map/ppermute | solution.py:162
  48.0 12.0 %collective-permute-start.14 = (f32[48,768]{1,0:T(8,128)S(1)}, f32[48,768]{1,0:T(8,128)S(1)}, u32[]{:S(2)}, u32[]{:S(2)}) collective-permute-start(f32[48,768]{1,0:T(8,128)S(1)} %get-tuple-element.17.w_ref), channel_id=1, source_target_pairs={{1,2},{2,1},{3,4},{4,3},{5,6},{6,5},{7,0},{0,7},{9,10},{10,9},{11,... | collective-permute-start | bytes 442376 | tf_op jit(solution)/shard_map/ppermute | solution.py:162
  51.1 4.4 %collective-permute-start.15 = (f32[48,384]{1,0:T(8,128)S(1)}, f32[48,384]{1,0:T(8,128)S(1)}, u32[]{:S(2)}, u32[]{:S(2)}) collective-permute-start(f32[48,384]{1,0:T(8,128)S(1)} %get-tuple-element.18), channel_id=1, source_target_pairs={{0,16},{16,0},{1,17},{17,1},{2,18},{18,2},{3,19},{19,3},{4,20},{20... | collective-permute-start | bytes 221192 | tf_op jit(solution)/shard_map/ppermute | solution.py:162
  52.0 7.9 %collective-permute-start.16 = (f32[48,384]{1,0:T(8,128)S(1)}, f32[48,384]{1,0:T(8,128)S(1)}, u32[]{:S(2)}, u32[]{:S(2)}) collective-permute-start(f32[48,384]{1,0:T(8,128)S(1)} %get-tuple-element.18), channel_id=1, source_target_pairs={{0,17},{17,0},{1,18},{18,1},{2,19},{19,2},{3,20},{20,3},{4,21},{21... | collective-permute-start | bytes 221192 | tf_op jit(solution)/shard_map/ppermute | solution.py:162
  60.2 3.7 %collective-permute-start.17 = (f32[48,768]{1,0:T(8,128)S(1)}, f32[48,768]{1,0:T(8,128)S(1)}, u32[]{:S(2)}, u32[]{:S(2)}) collective-permute-start(f32[48,768]{1,0:T(8,128)S(1)} %get-tuple-element.19.w_ref), channel_id=1, source_target_pairs={{0,8},{8,0},{1,9},{9,1},{2,10},{10,2},{3,11},{11,3},{4,12},{12,4},... | collective-permute-start | bytes 442376 | tf_op jit(solution)/shard_map/ppermute | solution.py:162
  60.3 11.6 %collective-permute-start.18 = (f32[48,768]{1,0:T(8,128)S(1)}, f32[48,768]{1,0:T(8,128)S(1)}, u32[]{:S(2)}, u32[]{:S(2)}) collective-permute-start(f32[48,768]{1,0:T(8,128)S(1)} %get-tuple-element.19.w_ref), channel_id=1, source_target_pairs={{0,1},{1,0},{2,3},{3,2},{4,5},{5,4},{6,7},{7,6},{8,9},{9,8},{10,11... | collective-permute-start | bytes 442376 | tf_op jit(solution)/shard_map/ppermute | solution.py:162
  60.4 11.5 %collective-permute-start.19 = (f32[48,768]{1,0:T(8,128)S(1)}, f32[48,768]{1,0:T(8,128)S(1)}, u32[]{:S(2)}, u32[]{:S(2)}) collective-permute-start(f32[48,768]{1,0:T(8,128)S(1)} %get-tuple-element.19.w_ref), channel_id=1, source_target_pairs={{1,2},{2,1},{3,4},{4,3},{5,6},{6,5},{7,0},{0,7},{9,10},{10,9},{11,... | collective-permute-start | bytes 442376 | tf_op jit(solution)/shard_map/ppermute | solution.py:162
  63.0 4.4 %collective-permute-start.20 = (f32[48,384]{1,0:T(8,128)S(1)}, f32[48,384]{1,0:T(8,128)S(1)}, u32[]{:S(2)}, u32[]{:S(2)}) collective-permute-start(f32[48,384]{1,0:T(8,128)S(1)} %get-tuple-element.20), channel_id=1, source_target_pairs={{0,16},{16,0},{1,17},{17,1},{2,18},{18,2},{3,19},{19,3},{4,20},{20... | collective-permute-start | bytes 221192 | tf_op jit(solution)/shard_map/ppermute | solution.py:162
  63.9 7.9 %collective-permute-start.21 = (f32[48,384]{1,0:T(8,128)S(1)}, f32[48,384]{1,0:T(8,128)S(1)}, u32[]{:S(2)}, u32[]{:S(2)}) collective-permute-start(f32[48,384]{1,0:T(8,128)S(1)} %get-tuple-element.20), channel_id=1, source_target_pairs={{0,17},{17,0},{1,18},{18,1},{2,19},{19,2},{3,20},{20,3},{4,21},{21... | collective-permute-start | bytes 221192 | tf_op jit(solution)/shard_map/ppermute | solution.py:162
  72.2 1.3 %collective-permute-start.22 = (f32[48,384]{1,0:T(8,128)S(1)}, f32[48,384]{1,0:T(8,128)S(1)}, u32[]{:S(2)}, u32[]{:S(2)}) collective-permute-start(f32[48,384]{1,0:T(8,128)S(1)} %slice_select_fusion), channel_id=1, source_target_pairs={{0,8},{8,0},{1,9},{9,1},{2,10},{10,2},{3,11},{11,3},{4,12},{12,4},... | collective-permute-start | bytes 221192 | tf_op jit(solution)/shard_map/ppermute | solution.py:162
  (18 other events, 67.6 us)

commit v2 on v1

--- a/solution.py
+++ b/solution.py
@@ -37,43 +37,25 @@
     )
 
 
-def block_plan(groups, slots):
+def block_plan(groups, slots, base, rise, place):
     blocks = groups * slots * 2
     rows = []
     for k in range(blocks):
         for e in range(blocks):
             d = (e + k) % blocks
             dest, source = d // 2, e // 2
-            rows.append((dest, source % slots, source // slots - dest // slots, d % 2, e % 2, float(d == e)))
+            climb = source // slots - dest // slots
+            name = (base + (rise if climb else 0)) * slots + source % slots
+            straight = d % 2 == e % 2
+            rows.append((dest + place * slots, name, climb, 0 if straight else e % 2 - d % 2, d == e and base == 0))
     return np.array(rows, np.float32)
 
 
-def weights_of(plan, info, base, rise, role_up, role_down, flip, strength, slots):
-    modes = strength.shape[1]
-    dest = plan[:, 0].astype(np.int32)
-    pick = np.eye(info.shape[0], dtype=np.float32)[dest]
-    local = jnp.dot(pick, info, precision=HIGHEST)
-    level, up, down = local[:, :modes], local[:, modes : 2 * modes], local[:, 2 * modes :]
-    same = (plan[:, 2:3] == 0).astype(np.float32)
-    name = (base + rise * (1 - same)) * slots + plan[:, 1:2]
-    climb = plan[:, 2:3] * flip
-    go_up = role_up * jnp.maximum(same, (climb == 1).astype(jnp.float32))
-    go_down = role_down * jnp.maximum(same, (climb == -1).astype(jnp.float32))
-    ups = go_up * (up == name)
-    downs = go_down * (down == name) * level
-    gap = ups + downs * strength[0][None, :]
-    plus = downs * strength[1][None, :]
-    straight = plan[:, 3:4] == plan[:, 4:5]
-    sign = plan[:, 4:5] - plan[:, 3:4]
-    return jnp.where(straight, plus, sign * gap), jnp.where(straight, plus, -sign * gap), level
-
-
-def table_of(row_part, column_part, blocks, width):
-    spread = np.kron(np.eye(blocks, dtype=np.float32), np.ones((1, width), np.float32))
-    groups = row_part.shape[0] // blocks
-    rows = row_part.reshape(groups, blocks, -1)
-    wide = jnp.einsum("gea,el->gal", rows, spread, precision=HIGHEST)
-    return wide + column_part.reshape(groups, 1, blocks * width)
+def setup_plan(slots, edges):
+    slabs = [block_plan(2, slots, base, 1, 0) for base in (0, 2, 2)]
+    for place in edges:
+        slabs += [block_plan(1, slots, base, 0, place) for base in (1, 3)]
+    return slabs
 
 
 def turned(value, steps, width):
@@ -85,12 +67,108 @@
     return jnp.concatenate([value[:, half:], value[:, :half]], 1)
 
 
-def own_kernel(step, width, w_ref, other_ref, start_ref, near_ref, far_ref, right_ref, table_ref, out_ref, comm_ref):
+def setup_kernel(slabs, links, chips, width, plan_ref, pick_ref, info_ref, ham_ref, coup_ref, base_ref, strength_ref, *outs):
+    count = len(slabs)
+    tables, (ham_out, right_out), (beta_ref, wide_ref, edge_ref) = outs[:count], outs[count : count + 2], outs[count + 2 :]
+    tier, mode = lax.axis_index("tier"), lax.axis_index("mode")
+    core, chip = tier % 2, tier // 2
+    flip = (1 - 2 * (chip % 2)).astype(jnp.float32)
+
+    def flag(test):
+        return test.astype(jnp.float32)
+
+    roles = [(jnp.float32(1), jnp.float32(1))]
+    for p in (0, 1):
+        ahead = flag(mode % 2 == p)
+        roles.append((ahead, 1.0 - ahead))
+    for p in links:
+        lower = flag((chip % 2 == p) & (chip + 1 < chips))
+        upper = flag((chip % 2 != p) & (chip >= 1))
+        roles += [(lower, upper), (lower, upper)]
+
+    size = ham_ref.shape[0]
+    half = size // 2
+    wide = coup_ref.shape[0]
+    strong, weak = strength_ref[0:1, :], strength_ref[1:2, :]
+    level = jnp.dot(pick_ref[...], info_ref[0], precision=HIGHEST, preferred_element_type=jnp.float32)
+    ups = jnp.dot(pick_ref[...], info_ref[1], precision=HIGHEST, preferred_element_type=jnp.float32)
+    downs = jnp.dot(pick_ref[...], info_ref[2], precision=HIGHEST, preferred_element_type=jnp.float32)
+    row_w, col_w = [], []
+    at = 0
+    for slab, (up, down) in zip(slabs, roles):
+        part = slice(at, at + len(slab))
+        at += len(slab)
+        name, climb, sign = plan_ref[0, part, :], plan_ref[1, part, :] * flip, plan_ref[2, part, :]
+        same = plan_ref[1, part, :] == 0.0
+        go_up = jnp.where(same | (climb == 1.0), up, 0.0)
+        go_down = jnp.where(same | (climb == -1.0), down, 0.0)
+        rise = jnp.where(ups[part] == name, go_up, 0.0)
+        fall = jnp.where(downs[part] == name, go_down, 0.0) * level[part]
+        gap = sign * (rise + fall * strong)
+        plus = fall * weak
+        straight = sign == 0.0
+        row_w.append(jnp.where(straight, plus, gap))
+        col_w.append(jnp.where(straight, plus, -gap))
+    row_w = jnp.concatenate(row_w, 0)
+    drain = -plan_ref[3] * level
+    mine = base_ref[pl.ds(pl.multiple_of(core * half, 8), half), :]
+    contract = (((1,), (1,)), ((), ()))
+    alpha = lax.dot_general(mine[:, :wide], row_w, contract, precision=HIGHEST, preferred_element_type=jnp.float32)
+    alpha += lax.dot_general(mine[:, wide:], drain, contract, precision=HIGHEST, preferred_element_type=jnp.float32)
+    beta_ref[...] = jnp.dot(jnp.concatenate(col_w, 0), coup_ref[...], precision=HIGHEST, preferred_element_type=jnp.float32)
+    blocks = tables[0].shape[0]
+    full_rows = 3 * blocks
+    for e in range(blocks):
+        wide_ref[:, e * width : (e + 1) * width] = beta_ref[pl.ds(e, full_rows, stride=blocks), :]
+    small = blocks // 2
+    edge_rows = (count - 3) * small
+    first_edge = full_rows * blocks
+    for e in range(small):
+        if edge_rows:
+            edge_ref[:, e * width : (e + 1) * width] = beta_ref[pl.ds(first_edge + e, edge_rows, stride=small), :]
+    lane = lax.broadcasted_iota(jnp.int32, (8, 128), 1)
+    at = 0
+    for n, table in enumerate(tables):
+        rolls = table.shape[0]
+        for k in range(rolls):
+            row = (n * blocks + k) if n < 3 else (n - 3) * small + k
+            beta = wide_ref if n < 3 else edge_ref
+            for a in range(0, half, 8):
+                for v in range(table.shape[2] // 128):
+                    e1, e2 = 128 * v // width, (128 * v + 127) // width
+                    value = alpha[a : a + 8, at + e1 : at + e1 + 1]
+                    if e2 > e1:
+                        later = alpha[a : a + 8, at + e2 : at + e2 + 1]
+                        value = jnp.where(lane < e2 * width - 128 * v, value, later)
+                    table[k, a : a + 8, 128 * v : 128 * v + 128] = value + beta[row : row + 1, 128 * v : 128 * v + 128]
+            at += rolls
+    ham = 0.5 * (ham_ref[...] + ham_ref[...].T)
+    beta_ref[0:size, :] = ham
+    own = beta_ref[pl.ds(pl.multiple_of(core * half, 8), half), :]
+    ham_out[...] = jnp.where(core == 0, own, jnp.concatenate([own[:, half:], own[:, :half]], 1))
+    right_out[...] = jnp.zeros_like(right_out)
+    for e in range(right_out.shape[0] // size):
+        right_out[e * size : (e + 1) * size, e * size : (e + 1) * size] = ham
+
+
+def assemble_kernel(edges, keep_ref, got_ref, out_ref, *edge_refs):
+    tier = lax.axis_index("tier")
+    first = ((tier % 2) ^ ((tier // 2) % 2)) == 0
+    lanes = keep_ref.shape[1]
+    keep, got = keep_ref[...], got_ref[...]
+    halves = [jnp.where(first, keep, got), jnp.where(first, got, keep)]
+    out_ref[:, :lanes] = halves[0]
+    out_ref[:, lanes:] = halves[1]
+    for n, place in enumerate(edges):
+        edge_refs[n][...] = halves[place]
+
+
+def own_kernel(step, width, w_ref, other_ref, start_ref, ham_ref, right_ref, table_ref, out_ref, comm_ref):
     rows, lanes = w_ref.shape
     half = lanes // 2
     w = w_ref[...]
-    left = jnp.dot(near_ref[...], w, precision=HIGHEST, preferred_element_type=jnp.float32)
-    left += jnp.dot(far_ref[...], other_ref[...], precision=HIGHEST, preferred_element_type=jnp.float32)
+    both = jnp.concatenate([w, other_ref[...]], 0)
+    left = jnp.dot(ham_ref[...], both, precision=HIGHEST, preferred_element_type=jnp.float32)
     stacked = jnp.concatenate([w[:, :half], w[:, half:]], 0)
     right = jnp.dot(stacked, right_ref[...], precision=HIGHEST, preferred_element_type=jnp.float32)
     comm_ref[:, :half] = left[:, :half] - right[:rows]
@@ -155,75 +233,61 @@
     half, lanes = size // 2, slots * 2 * size
     tier, mode = lax.axis_index("tier"), lax.axis_index("mode")
     core, chip = tier % 2, tier // 2
-    turn = chip % 2
-    place = core ^ turn
+    place = core ^ (chip % 2)
 
     def send(value, route):
         return lax.ppermute(value, AXES, route)
 
+    facts = jnp.stack([a.reshape(a.shape[2:]) for a in (occupancy, up_index, down_index)])
+    other_facts = send(facts, core_route)
     own = ados.reshape(slots * 2, size, size).transpose(1, 0, 2).reshape(size, lanes)
     keep = lax.dynamic_slice(own, (core * half, 0), (half, lanes))
     got = send(lax.dynamic_slice(own, ((1 - core) * half, 0), (half, lanes)), core_route)
     first = place == 0
-    start = jnp.concatenate([jnp.where(first, keep, got), jnp.where(first, got, keep)], 1)
-
-    facts = [a.reshape(a.shape[2:]).astype(jnp.float32) for a in (occupancy, up_index, down_index)]
-    info = jnp.concatenate(facts, 1)
-    other_info = send(info, core_route)
-    info = jnp.concatenate([jnp.where(first, info, other_info), jnp.where(first, other_info, info)], 0)
-    start, info = lax.optimization_barrier((start, info))
-
-    ham = 0.5 * (hamiltonian + hamiltonian.T)
-    mine = lax.dynamic_slice(ham, (core * half, 0), (half, size))
-    near = jnp.where(core == 0, mine[:, :half], mine[:, half:])
-    far = jnp.where(core == 0, mine[:, half:], mine[:, :half])
-    right = jnp.tile(ham, (2 * slots, 2 * slots)) * np.kron(
-        np.eye(2 * slots, dtype=np.float32), np.ones((size, size), np.float32)
-    )
-
-    flip = (1 - 2 * turn).astype(jnp.float32)
-    rows_c = lax.dynamic_slice(couplings, (0, core * half), (couplings.shape[0], half))
-    one = jnp.float32(1.0)
-    blocks = 4 * slots
-    plan = block_plan(2, slots)
-    sources = [(0.0, one, one)]
-    for p in (0, 1):
-        ahead = (mode % 2 == p).astype(jnp.float32)
-        sources.append((2.0, ahead, 1.0 - ahead))
-    row_w, col_w, damp = [], [], None
-    for base, up, down in sources:
-        a, b, level = weights_of(plan, info, base, 1.0, up, down, flip, strength, slots)
-        row_w.append(a)
-        col_w.append(b)
-        if damp is None:
-            damp = jnp.sum(level * rates[None, :], 1, keepdims=True) * plan[:, 5:6]
-    row_part = jnp.dot(jnp.concatenate(row_w, 0), rows_c, precision=HIGHEST)
-    row_part = jnp.concatenate([row_part[: damp.shape[0]] - damp, row_part[damp.shape[0] :]], 0)
-    column_part = jnp.dot(jnp.concatenate(col_w, 0), couplings, precision=HIGHEST)
-    tables = table_of(row_part, column_part, blocks, size).reshape(3, blocks, half, 2 * lanes)
-    tables = [tables[0], tables[1], tables[2]]
-
-    edge_plan = block_plan(1, slots)
     links = [p for p in (0, 1) if flat_routes[p]]
     edges = tuple(1 - p for p in links)
-    edge_tables = []
-    for p in links:
-        lower = (chip % 2 == p) & (chip + 1 < tiers // 2)
-        upper = (chip % 2 != p) & (chip >= 1)
-        up, down = lower.astype(jnp.float32), upper.astype(jnp.float32)
-        where = (1 - p) * slots
-        pair = []
-        for base in (1.0, 3.0):
-            a, b, _ = weights_of(edge_plan, info[where : where + slots], base, 0.0, up, down, flip, strength, slots)
-            row_part = jnp.dot(a, rows_c, precision=HIGHEST)
-            column_part = jnp.dot(b, couplings, precision=HIGHEST)
-            pair.append(table_of(row_part, column_part, blocks // 2, size))
-        edge_tables.append(pair)
-
     full = jax.ShapeDtypeStruct((half, 2 * lanes), jnp.float32)
     edge = jax.ShapeDtypeStruct((half, lanes), jnp.float32)
+    start, *brink = pl.pallas_call(
+        functools.partial(assemble_kernel, edges),
+        out_shape=[full] + [edge] * len(links),
+        in_specs=[VMEM] * 2,
+        out_specs=[VMEM] * (1 + len(links)),
+        compiler_params=GRANT,
+        name="assemble",
+    )(keep, got)
+
+    late = (start, facts, other_facts, hamiltonian, couplings, rates, strength)
+    start, facts, other_facts, hamiltonian, couplings, rates, strength = lax.optimization_barrier(late)
+    info = jnp.concatenate([jnp.where(first, facts, other_facts), jnp.where(first, other_facts, facts)], 1)
+    info = info.astype(jnp.float32)
+    slabs = setup_plan(slots, edges)
+    plan = np.concatenate(slabs, 0)
+    bath = couplings.shape[0]
+    pick = np.eye(2 * slots, dtype=np.float32)[plan[:, 0].astype(np.int32)]
+    plan = np.broadcast_to(plan.T[1:, :, None], (4, plan.shape[0], bath)).copy()
+    base = jnp.concatenate([couplings.T, jnp.broadcast_to(rates[None, :], (size, bath))], 1)
+    blocks = 4 * slots
+    big = jax.ShapeDtypeStruct((blocks, half, 2 * lanes), jnp.float32)
+    small = jax.ShapeDtypeStruct((blocks // 2, half, lanes), jnp.float32)
+    edge_count = 2 * len(links)
+    *tables, ham, right = pl.pallas_call(
+        functools.partial(setup_kernel, slabs, links, tiers // 2, size),
+        out_shape=[big] * 3
+        + [small] * edge_count
+        + [jax.ShapeDtypeStruct((half, size), jnp.float32), jax.ShapeDtypeStruct((lanes, lanes), jnp.float32)],
+        in_specs=[VMEM] * 7,
+        out_specs=[VMEM] * (5 + edge_count),
+        scratch_shapes=[
+            pltpu.VMEM((plan.shape[1], size), jnp.float32),
+            pltpu.VMEM((3 * blocks, 2 * lanes), jnp.float32),
+            pltpu.VMEM((max(edge_count * blocks // 2, 8), lanes), jnp.float32),
+        ],
+        compiler_params=GRANT,
+        name="setup",
+    )(plan, pick, info, hamiltonian, couplings, base, strength)
+
     w = start
-    brink = [start[:, q * lanes : (q + 1) * lanes] for q in edges]
     for stage in (4, 3, 2, 1):
         step = TIME_STEP / stage
         flat = [send(brink[n], flat_routes[p]) for n, p in enumerate(links)]
@@ -234,13 +298,13 @@
         part = pl.pallas_call(
             functools.partial(own_kernel, step, size),
             out_shape=full,
-            in_specs=[VMEM] * 7,
+            in_specs=[VMEM] * 6,
             out_specs=VMEM,
             scratch_shapes=[pltpu.VMEM((half, 2 * lanes), jnp.float32)],
             compiler_params=GRANT,
             name="own_part",
-        )(w, other, start, near, far, right, tables[0])
-        extra = [a for n in range(len(links)) for a in (flat[n], slant[n], *edge_tables[n])]
+        )(w, other, start, ham, right, tables[0])
+        extra = [a for n in range(len(links)) for a in (flat[n], slant[n], *tables[3 + 2 * n : 5 + 2 * n])]
         count = len(links) if stage > 1 else 0
         result = pl.pallas_call(
             functools.partial(link_kernel, step, size, edges),

time: 75.3 us -> 57.5 us (0.76)
  matrix products: 9.35 us -> 0 us
  local copies, waits for them, and re-layouts: 9.89 us -> 2.77 us
  waiting for transfers between devices: 19.1 us -> 25.4 us
  other arithmetic: 3.57 us -> 0.14 us
  starting transfers between devices: 22.6 us -> 20.9 us
  Pallas kernels: 9.41 us -> 7.79 us
    dot_general x11 -> x0, matrix products: 9.35 us -> none  [the longest x3 5.64 us: table_of(): wide = jnp.einsum('gea,el->gal', rows, spread, precision=HIGHEST)]
    ppermute x23, waiting for transfers between devices: 19.1 us -> 25.4 us  [send(): return lax.ppermute(value, AXES, route)]
    pallas_call x4, Pallas kernels: 7.08 us -> 3.07 us  [shards(): pl.pallas_call(functools.partial(own_kernel, step, size), out_shape=full,...]
    pallas_call x0 -> x2, Pallas kernels: none -> 3.48 us  [the longest x1 3.46 us: shards(): pl.pallas_call(functools.partial(setup_kernel, slabs, links, tiers // 2,...]
    unnamed x55 -> x18, local copies, waits for them, and re-layouts: 2.75 us -> 0.04 us
    slice x3 -> x0, local copies, waits for them, and re-layouts: 1.85 us -> none  [the longest x1 1.54 us: shards(): brink = [start[:, q * lanes:(q + 1) * lanes] for q in edges]]
    ppermute x23, starting transfers between devices: 22.6 us -> 20.9 us  [send(): return lax.ppermute(value, AXES, route)]
    add x3 -> x0, local copies, waits for them, and re-layouts: 1.52 us -> none  [table_of(): return wide + column_part.reshape(groups, 1, blocks * width)]
  transfers between devices with their start and end apart: 23 -> 23, of which waited for: 7 -> 10; matrix products, arithmetic and copies ran while one was open for 19% -> 0% of each run, Pallas kernels for 9% -> 11%
where the time goes in v2:
time: 57.5 us; the launch traced here: 57.3 us
  waiting for transfers between devices  25.4 us (44%)
  starting transfers between devices  20.9 us (36%)
  Pallas kernels  7.79 us (14%)
  local copies, waits for them, and re-layouts  2.77 us (5%)
    ppermute x23, waiting for transfers between devices, send(): return lax.ppermute(value, AXES, route)  25.4 us
    ppermute x23, starting transfers between devices, send(): return lax.ppermute(value, AXES, route)  20.9 us
    pallas_call x1, Pallas kernels, shards(): pl.pallas_call(functools.partial(setup_kernel, slabs, links, tiers // 2,...  3.46 us
    pallas_call x4, Pallas kernels, shards(): pl.pallas_call(functools.partial(own_kernel, step, size), out_shape=full,...  3.07 us
    reshape x3, local copies, waits for them, and re-layouts, shards(): ados.reshape(slots * 2, size, size).transpose(1, 0, 2).reshape(size, lanes)  1.48 us
    pallas_call x4, Pallas kernels, shards(): pl.pallas_call(functools.partial(link_kernel, step, size, edges), out_sha...  1.23 us
  transfers between devices with their start and end apart: 23, of which 10 were waited for; matrix products, arithmetic and copies ran while one was open for 0% of the time, Pallas kernels for 11%

profile of v2, /device:TPU:0, one launch (start us, length us, event | category | flops | bytes accessed | tf_op | source)
XLA Modules:
  0.0 57.3 jit_solution(6285584546887536849)
XLA Ops:
  0.1 1.2 %reshape.13 = f32[4,96,96]{2,1,0:T(8,128)S(1)} reshape(f32[1,1,2,2,9216]{4,3,2,1,0:T(2,128)} %param.10) | data formatting | bytes 294912 | tf_op jit(solution)/shard_map/reshape | solution.py:243
  1.6 0.6 %collective-permute-start = (f32[48,384]{1,0:T(8,128)S(1)}, f32[48,384]{1,0:T(8,128)S(1)}, u32[]{:S(2)}, u32[]{:S(2)}) collective-permute-start(f32[48,384]{1,0:T(8,128)S(1)} %get-tuple-element.51), channel_id=1, source_target_pairs={{0,8},{8,0},{1,9},{9,1},{2,10},{10,2},{3,11},{11,3},{4,12},{12,4},... | collective-permute-start | bytes 221192 | tf_op jit(solution)/shard_map/ppermute | solution.py:239
  2.3 0.8 %collective-permute-done.got_ref = f32[48,384]{1,0:T(8,128)S(1)} collective-permute-done((f32[48,384]{1,0:T(8,128)S(1)}, f32[48,384]{1,0:T(8,128)S(1)}, u32[]{:S(2)}, u32[]{:S(2)}) %collective-permute-start) | collective-permute-done | bytes 73760 | tf_op jit(solution)/shard_map/ppermute | solution.py:239
  3.1 0.3 collective-permute-done.1
  3.6 2.8 %collective-permute-start.3 = (f32[48,768]{1,0:T(8,128)S(1)}, f32[48,768]{1,0:T(8,128)S(1)}, u32[]{:S(2)}, u32[]{:S(2)}) collective-permute-start(f32[48,768]{1,0:T(8,128)S(1)} %get-tuple-element.28.w_ref.start_ref), channel_id=1, source_target_pairs={{0,1},{1,0},{2,3},{3,2},{4,5},{5,4},{6,7},{7,6},{8,9},{9,8},{10,11... | collective-permute-start | bytes 442376 | tf_op jit(solution)/shard_map/ppermute | solution.py:239
  6.4 3.6 %collective-permute-start.4 = (f32[48,768]{1,0:T(8,128)S(1)}, f32[48,768]{1,0:T(8,128)S(1)}, u32[]{:S(2)}, u32[]{:S(2)}) collective-permute-start(f32[48,768]{1,0:T(8,128)S(1)} %get-tuple-element.28.w_ref.start_ref), channel_id=1, source_target_pairs={{1,2},{2,1},{3,4},{4,3},{5,6},{6,5},{7,0},{0,7},{9,10},{10,9},{11,... | collective-permute-start | bytes 442376 | tf_op jit(solution)/shard_map/ppermute | solution.py:239
  10.0 1.5 %collective-permute-start.5 = (f32[48,384]{1,0:T(8,128)S(1)}, f32[48,384]{1,0:T(8,128)S(1)}, u32[]{:S(2)}, u32[]{:S(2)}) collective-permute-start(f32[48,384]{1,0:T(8,128)S(1)} %get-tuple-element.40), channel_id=1, source_target_pairs={{0,16},{16,0},{1,17},{17,1},{2,18},{18,2},{3,19},{19,3},{4,20},{20... | collective-permute-start | bytes 221192 | tf_op jit(solution)/shard_map/ppermute | solution.py:239
  11.8 3.5 %setup.1 = (f32[8,48,768]{2,1,0:T(8,128)S(1)}, f32[8,48,768]{2,1,0:T(8,128)S(1)}, f32[8,48,768]{2,1,0:T(8,128)S(1)}, f32[4,48,384]{2,1,0:T(8,128)S(1)}, f32[4,48...) custom-call(f32[4,224,16]{2,1,0:T(8,128)S(1)} %copy-done, f32[224,4]{1,0:T(8,128)S(1)} %copy-done.1, ...), custom_call_target="tpu_custom_call" | custom-call | tf_op jit(solution)/shard_map/setup/pallas_call | solution.py:274
  15.3 0.8 %own_part.4.refs_0_ = f32[48,768]{1,0:T(8,128)S(1)} custom-call(f32[48,768]{1,0:T(8,128)S(1)} %get-tuple-element.28.w_ref.start_ref, f32[48,768]{1,0:T(8,128)S(1)} %collective-permute-done.2.other_ref, f32[48,768]{1,0:T(8,128)S(1)} %get-tuple-element.28.w_ref.start_ref, f32[48,96]{1,0:T(8,128)S(1)} %get-tuple-element.35.ham_ref, ...), custom_call_target="tpu_custom_call" | custom-call | tf_op jit(solution)/shard_map/own_part/pallas_call | solution.py:298
  16.1 1.2 %collective-permute-done.6.refs_6_ = f32[48,384]{1,0:T(8,128)S(1)} collective-permute-done((f32[48,384]{1,0:T(8,128)S(1)}, f32[48,384]{1,0:T(8,128)S(1)}, u32[]{:S(2)}, u32[]{:S(2)}) %collective-permute-start.6) | collective-permute-done | bytes 73760 | tf_op jit(solution)/shard_map/ppermute | solution.py:239
  17.3 0.3 link_part.4
  17.8 4.3 %collective-permute-start.9 = (f32[48,768]{1,0:T(8,128)S(1)}, f32[48,768]{1,0:T(8,128)S(1)}, u32[]{:S(2)}, u32[]{:S(2)}) collective-permute-start(f32[48,768]{1,0:T(8,128)S(1)} %get-tuple-element.43.w_ref), channel_id=1, source_target_pairs={{1,2},{2,1},{3,4},{4,3},{5,6},{6,5},{7,0},{0,7},{9,10},{10,9},{11,... | collective-permute-start | bytes 442376 | tf_op jit(solution)/shard_map/ppermute | solution.py:239
  22.1 0.4 collective-permute-start.10
  22.5 0.8 %own_part.5.refs_0_ = f32[48,768]{1,0:T(8,128)S(1)} custom-call(f32[48,768]{1,0:T(8,128)S(1)} %get-tuple-element.43.w_ref, f32[48,768]{1,0:T(8,128)S(1)} %collective-permute-done.7.other_ref, f32[48,768]{1,0:T(8,128)S(1)} %get-tuple-element.28.w_ref.start_ref, f32[48,96]{1,0:T(8,128)S(1)} %get-tuple-element.35.ham_ref, ...), custom_call_target="tpu_custom_call" | custom-call | tf_op jit(solution)/shard_map/own_part/pallas_call | solution.py:298
  23.2 3.2 %collective-permute-done.10.refs_5_ = f32[48,384]{1,0:T(8,128)S(1)} collective-permute-done((f32[48,384]{1,0:T(8,128)S(1)}, f32[48,384]{1,0:T(8,128)S(1)}, u32[]{:S(2)}, u32[]{:S(2)}) %collective-permute-start.10) | collective-permute-done | bytes 73760 | tf_op jit(solution)/shard_map/ppermute | solution.py:239
  26.5 4.3 %collective-permute-done.11.refs_6_ = f32[48,384]{1,0:T(8,128)S(1)} collective-permute-done((f32[48,384]{1,0:T(8,128)S(1)}, f32[48,384]{1,0:T(8,128)S(1)}, u32[]{:S(2)}, u32[]{:S(2)}) %collective-permute-start.11) | collective-permute-done | bytes 73760 | tf_op jit(solution)/shard_map/ppermute | solution.py:239
  30.8 0.3 link_part.5
  31.3 2.5 %collective-permute-start.14 = (f32[48,768]{1,0:T(8,128)S(1)}, f32[48,768]{1,0:T(8,128)S(1)}, u32[]{:S(2)}, u32[]{:S(2)}) collective-permute-start(f32[48,768]{1,0:T(8,128)S(1)} %get-tuple-element.45.w_ref), channel_id=1, source_target_pairs={{1,2},{2,1},{3,4},{4,3},{5,6},{6,5},{7,0},{0,7},{9,10},{10,9},{11,... | collective-permute-start | bytes 442376 | tf_op jit(solution)/shard_map/ppermute | solution.py:239
  33.7 0.6 %collective-permute-start.15 = (f32[48,384]{1,0:T(8,128)S(1)}, f32[48,384]{1,0:T(8,128)S(1)}, u32[]{:S(2)}, u32[]{:S(2)}) collective-permute-start(f32[48,384]{1,0:T(8,128)S(1)} %get-tuple-element.46), channel_id=1, source_target_pairs={{0,16},{16,0},{1,17},{17,1},{2,18},{18,2},{3,19},{19,3},{4,20},{20... | collective-permute-start | bytes 221192 | tf_op jit(solution)/shard_map/ppermute | solution.py:239
  34.4 0.4 collective-permute-start.16
  34.8 0.8 %own_part.6.refs_0_ = f32[48,768]{1,0:T(8,128)S(1)} custom-call(f32[48,768]{1,0:T(8,128)S(1)} %get-tuple-element.45.w_ref, f32[48,768]{1,0:T(8,128)S(1)} %collective-permute-done.12.other_ref, f32[48,768]{1,0:T(8,128)S(1)} %get-tuple-element.28.w_ref.start_ref, f32[48,96]{1,0:T(8,128)S(1)} %get-tuple-element.35.ham_ref, ...), custom_call_target="tpu_custom_call" | custom-call | tf_op jit(solution)/shard_map/own_part/pallas_call | solution.py:298
  35.5 2.6 %collective-permute-done.15.refs_5_ = f32[48,384]{1,0:T(8,128)S(1)} collective-permute-done((f32[48,384]{1,0:T(8,128)S(1)}, f32[48,384]{1,0:T(8,128)S(1)}, u32[]{:S(2)}, u32[]{:S(2)}) %collective-permute-start.15) | collective-permute-done | bytes 73760 | tf_op jit(solution)/shard_map/ppermute | solution.py:239
  38.2 4.7 %collective-permute-done.16.refs_6_ = f32[48,384]{1,0:T(8,128)S(1)} collective-permute-done((f32[48,384]{1,0:T(8,128)S(1)}, f32[48,384]{1,0:T(8,128)S(1)}, u32[]{:S(2)}, u32[]{:S(2)}) %collective-permute-start.16) | collective-permute-done | bytes 73760 | tf_op jit(solution)/shard_map/ppermute | solution.py:239
  42.9 0.3 link_part.6
  43.4 2.5 %collective-permute-start.19 = (f32[48,768]{1,0:T(8,128)S(1)}, f32[48,768]{1,0:T(8,128)S(1)}, u32[]{:S(2)}, u32[]{:S(2)}) collective-permute-start(f32[48,768]{1,0:T(8,128)S(1)} %get-tuple-element.47.w_ref), channel_id=1, source_target_pairs={{1,2},{2,1},{3,4},{4,3},{5,6},{6,5},{7,0},{0,7},{9,10},{10,9},{11,... | collective-permute-start | bytes 442376 | tf_op jit(solution)/shard_map/ppermute | solution.py:239
  45.8 0.8 %collective-permute-start.20 = (f32[48,384]{1,0:T(8,128)S(1)}, f32[48,384]{1,0:T(8,128)S(1)}, u32[]{:S(2)}, u32[]{:S(2)}) collective-permute-start(f32[48,384]{1,0:T(8,128)S(1)} %get-tuple-element.48), channel_id=1, source_target_pairs={{0,16},{16,0},{1,17},{17,1},{2,18},{18,2},{3,19},{19,3},{4,20},{20... | collective-permute-start | bytes 221192 | tf_op jit(solution)/shard_map/ppermute | solution.py:239
  46.9 0.8 %own_part.7.refs_0_ = f32[48,768]{1,0:T(8,128)S(1)} custom-call(f32[48,768]{1,0:T(8,128)S(1)} %get-tuple-element.47.w_ref, f32[48,768]{1,0:T(8,128)S(1)} %collective-permute-done.17.other_ref, f32[48,768]{1,0:T(8,128)S(1)} %get-tuple-element.28.w_ref.start_ref, f32[48,96]{1,0:T(8,128)S(1)} %get-tuple-element.35.ham_ref, ...), custom_call_target="tpu_custom_call" | custom-call | tf_op jit(solution)/shard_map/own_part/pallas_call | solution.py:298
  47.6 2.6 %collective-permute-done.20.refs_5_ = f32[48,384]{1,0:T(8,128)S(1)} collective-permute-done((f32[48,384]{1,0:T(8,128)S(1)}, f32[48,384]{1,0:T(8,128)S(1)}, u32[]{:S(2)}, u32[]{:S(2)}) %collective-permute-start.20) | collective-permute-done | bytes 73760 | tf_op jit(solution)/shard_map/ppermute | solution.py:239
  50.2 4.4 %collective-permute-done.21.refs_6_ = f32[48,384]{1,0:T(8,128)S(1)} collective-permute-done((f32[48,384]{1,0:T(8,128)S(1)}, f32[48,384]{1,0:T(8,128)S(1)}, u32[]{:S(2)}, u32[]{:S(2)}) %collective-permute-start.21) | collective-permute-done | bytes 73760 | tf_op jit(solution)/shard_map/ppermute | solution.py:239
  54.6 0.3 link_part.7
  55.0 1.2 %collective-permute-done.22 = f32[48,384]{1,0:T(8,128)S(1)} collective-permute-done((f32[48,384]{1,0:T(8,128)S(1)}, f32[48,384]{1,0:T(8,128)S(1)}, u32[]{:S(2)}, u32[]{:S(2)}) %collective-permute-start.22) | collective-permute-done | bytes 73760 | tf_op jit(solution)/shard_map/ppermute | solution.py:239
  56.4 0.9 %reshape.16 = f32[1,1,2,2,9216]{4,3,2,1,0:T(2,128)} reshape(f32[4,96,96]{2,1,0:T(8,128)S(1)} %copy.16) | data formatting | bytes 294912 | tf_op jit(solution)/shard_map/reshape | solution.py:323
  (58 shorter events, 1.9 us)
Async XLA Ops:
  0.0 11.8 %copy-start = (f32[4,224,16]{2,1,0:T(8,128)S(1)}, f32[4,224,16]{2,1,0:T(8,128)}, u32[]{:S(2)}) copy-start(f32[4,224,16]{2,1,0:T(8,128)} %constant.43.clone.plan_ref) | copy-start | bytes 172036
  0.0 11.8 %copy-start.1 = (f32[224,4]{1,0:T(8,128)S(1)}, f32[224,4]{1,0:T(8,128)}, u32[]{:S(2)}) copy-start(f32[224,4]{1,0:T(8,128)} %constant.44.clone.pick_ref) | copy-start | bytes 10756
  0.0 2.2 %copy-start.7 = (s32[1,1,2,16]{3,2,1,0:T(2,128)S(1)}, s32[1,1,2,16]{3,2,1,0:T(2,128)}, u32[]{:S(2)}) copy-start(s32[1,1,2,16]{3,2,1,0:T(2,128)} %param.15) | copy-start | bytes 388
  0.0 2.2 %copy-start.6 = (s32[1,1,2,16]{3,2,1,0:T(2,128)S(1)}, s32[1,1,2,16]{3,2,1,0:T(2,128)}, u32[]{:S(2)}) copy-start(s32[1,1,2,16]{3,2,1,0:T(2,128)} %param.16) | copy-start | bytes 388
  0.0 2.2 %copy-start.5 = (s32[1,1,2,16]{3,2,1,0:T(2,128)S(1)}, s32[1,1,2,16]{3,2,1,0:T(2,128)}, u32[]{:S(2)}) copy-start(s32[1,1,2,16]{3,2,1,0:T(2,128)} %param.17) | copy-start | bytes 388
  0.0 11.8 %copy-start.2 = (f32[96,96]{1,0:T(8,128)S(1)}, f32[96,96]{1,0:T(8,128)}, u32[]{:S(2)}) copy-start(f32[96,96]{1,0:T(8,128)} %ham_ref) | copy-start | bytes 110596
  0.0 11.6 %copy-start.3 = (f32[16,96]{1,0:T(8,128)S(1)}, f32[16,96]{1,0:T(8,128)}, u32[]{:S(2)}) copy-start(f32[16,96]{1,0:T(8,128)} %coup_ref) | copy-start | bytes 18436
  0.0 11.5 %copy-start.8 = (f32[16]{0:T(128)S(1)}, f32[16]{0:T(128)}, u32[]{:S(2)}) copy-start(f32[16]{0:T(128)} %param.13) | copy-start | bytes 196
  0.0 11.8 %copy-start.4 = (f32[2,16]{1,0:T(2,128)S(1)}, f32[2,16]{1,0:T(2,128)}, u32[]{:S(2)}) copy-start(f32[2,16]{1,0:T(2,128)} %strength_ref) | copy-start | bytes 388
  1.6 1.5 %collective-permute-start = (f32[48,384]{1,0:T(8,128)S(1)}, f32[48,384]{1,0:T(8,128)S(1)}, u32[]{:S(2)}, u32[]{:S(2)}) collective-permute-start(f32[48,384]{1,0:T(8,128)S(1)} %get-tuple-element.51), channel_id=1, source_target_pairs={{0,8},{8,0},{1,9},{9,1},{2,10},{10,2},{3,11},{11,3},{4,12},{12,4},... | collective-permute-start | bytes 221192 | tf_op jit(solution)/shard_map/ppermute | solution.py:239
  2.2 1.2 %collective-permute-start.1 = (s32[3,2,16]{2,1,0:T(2,128)S(1)}, s32[3,2,16]{2,1,0:T(2,128)S(1)}, u32[]{:S(2)}, u32[]{:S(2)}) collective-permute-start(s32[3,2,16]{2,1,0:T(2,128)S(1)} %pad_add_fusion), channel_id=1, source_target_pairs={{0,8},{8,0},{1,9},{9,1},{2,10},{10,2},{3,11},{11,3},{4,12},{12,4},... | collective-permute-start | bytes 1160 | tf_op jit(solution)/shard_map/ppermute | solution.py:239
  3.4 11.9 %collective-permute-start.2 = (f32[48,768]{1,0:T(8,128)S(1)}, f32[48,768]{1,0:T(8,128)S(1)}, u32[]{:S(2)}, u32[]{:S(2)}) collective-permute-start(f32[48,768]{1,0:T(8,128)S(1)} %get-tuple-element.28.w_ref.start_ref), channel_id=1, source_target_pairs={{0,8},{8,0},{1,9},{9,1},{2,10},{10,2},{3,11},{11,3},{4,12},{12,4},... | collective-permute-start | bytes 442376 | tf_op jit(solution)/shard_map/ppermute | solution.py:239
  3.6 13.7 %collective-permute-start.3 = (f32[48,768]{1,0:T(8,128)S(1)}, f32[48,768]{1,0:T(8,128)S(1)}, u32[]{:S(2)}, u32[]{:S(2)}) collective-permute-start(f32[48,768]{1,0:T(8,128)S(1)} %get-tuple-element.28.w_ref.start_ref), channel_id=1, source_target_pairs={{0,1},{1,0},{2,3},{3,2},{4,5},{5,4},{6,7},{7,6},{8,9},{9,8},{10,11... | collective-permute-start | bytes 442376 | tf_op jit(solution)/shard_map/ppermute | solution.py:239
  6.4 10.9 %collective-permute-start.4 = (f32[48,768]{1,0:T(8,128)S(1)}, f32[48,768]{1,0:T(8,128)S(1)}, u32[]{:S(2)}, u32[]{:S(2)}) collective-permute-start(f32[48,768]{1,0:T(8,128)S(1)} %get-tuple-element.28.w_ref.start_ref), channel_id=1, source_target_pairs={{1,2},{2,1},{3,4},{4,3},{5,6},{6,5},{7,0},{0,7},{9,10},{10,9},{11,... | collective-permute-start | bytes 442376 | tf_op jit(solution)/shard_map/ppermute | solution.py:239
  10.0 6.1 %collective-permute-start.5 = (f32[48,384]{1,0:T(8,128)S(1)}, f32[48,384]{1,0:T(8,128)S(1)}, u32[]{:S(2)}, u32[]{:S(2)}) collective-permute-start(f32[48,384]{1,0:T(8,128)S(1)} %get-tuple-element.40), channel_id=1, source_target_pairs={{0,16},{16,0},{1,17},{17,1},{2,18},{18,2},{3,19},{19,3},{4,20},{20... | collective-permute-start | bytes 221192 | tf_op jit(solution)/shard_map/ppermute | solution.py:239
  11.5 5.8 %collective-permute-start.6 = (f32[48,384]{1,0:T(8,128)S(1)}, f32[48,384]{1,0:T(8,128)S(1)}, u32[]{:S(2)}, u32[]{:S(2)}) collective-permute-start(f32[48,384]{1,0:T(8,128)S(1)} %get-tuple-element.40), channel_id=1, source_target_pairs={{0,17},{17,0},{1,18},{18,1},{2,19},{19,2},{3,20},{20,3},{4,21},{21... | collective-permute-start | bytes 221192 | tf_op jit(solution)/shard_map/ppermute | solution.py:239
  17.6 4.8 %collective-permute-start.7 = (f32[48,768]{1,0:T(8,128)S(1)}, f32[48,768]{1,0:T(8,128)S(1)}, u32[]{:S(2)}, u32[]{:S(2)}) collective-permute-start(f32[48,768]{1,0:T(8,128)S(1)} %get-tuple-element.43.w_ref), channel_id=1, source_target_pairs={{0,8},{8,0},{1,9},{9,1},{2,10},{10,2},{3,11},{11,3},{4,12},{12,4},... | collective-permute-start | bytes 442376 | tf_op jit(solution)/shard_map/ppermute | solution.py:239
  17.7 13.1 %collective-permute-start.8 = (f32[48,768]{1,0:T(8,128)S(1)}, f32[48,768]{1,0:T(8,128)S(1)}, u32[]{:S(2)}, u32[]{:S(2)}) collective-permute-start(f32[48,768]{1,0:T(8,128)S(1)} %get-tuple-element.43.w_ref), channel_id=1, source_target_pairs={{0,1},{1,0},{2,3},{3,2},{4,5},{5,4},{6,7},{7,6},{8,9},{9,8},{10,11... | collective-permute-start | bytes 442376 | tf_op jit(solution)/shard_map/ppermute | solution.py:239
  17.8 13.0 %collective-permute-start.9 = (f32[48,768]{1,0:T(8,128)S(1)}, f32[48,768]{1,0:T(8,128)S(1)}, u32[]{:S(2)}, u32[]{:S(2)}) collective-permute-start(f32[48,768]{1,0:T(8,128)S(1)} %get-tuple-element.43.w_ref), channel_id=1, source_target_pairs={{1,2},{2,1},{3,4},{4,3},{5,6},{6,5},{7,0},{0,7},{9,10},{10,9},{11,... | collective-permute-start | bytes 442376 | tf_op jit(solution)/shard_map/ppermute | solution.py:239
  22.1 4.4 %collective-permute-start.10 = (f32[48,384]{1,0:T(8,128)S(1)}, f32[48,384]{1,0:T(8,128)S(1)}, u32[]{:S(2)}, u32[]{:S(2)}) collective-permute-start(f32[48,384]{1,0:T(8,128)S(1)} %get-tuple-element.44), channel_id=1, source_target_pairs={{0,16},{16,0},{1,17},{17,1},{2,18},{18,2},{3,19},{19,3},{4,20},{20... | collective-permute-start | bytes 221192 | tf_op jit(solution)/shard_map/ppermute | solution.py:239
  22.5 8.3 %collective-permute-start.11 = (f32[48,384]{1,0:T(8,128)S(1)}, f32[48,384]{1,0:T(8,128)S(1)}, u32[]{:S(2)}, u32[]{:S(2)}) collective-permute-start(f32[48,384]{1,0:T(8,128)S(1)} %get-tuple-element.44), channel_id=1, source_target_pairs={{0,17},{17,0},{1,18},{18,1},{2,19},{19,2},{3,20},{20,3},{4,21},{21... | collective-permute-start | bytes 221192 | tf_op jit(solution)/shard_map/ppermute | solution.py:239
  31.1 3.6 %collective-permute-start.12 = (f32[48,768]{1,0:T(8,128)S(1)}, f32[48,768]{1,0:T(8,128)S(1)}, u32[]{:S(2)}, u32[]{:S(2)}) collective-permute-start(f32[48,768]{1,0:T(8,128)S(1)} %get-tuple-element.45.w_ref), channel_id=1, source_target_pairs={{0,8},{8,0},{1,9},{9,1},{2,10},{10,2},{3,11},{11,3},{4,12},{12,4},... | collective-permute-start | bytes 442376 | tf_op jit(solution)/shard_map/ppermute | solution.py:239
  31.2 11.7 %collective-permute-start.13 = (f32[48,768]{1,0:T(8,128)S(1)}, f32[48,768]{1,0:T(8,128)S(1)}, u32[]{:S(2)}, u32[]{:S(2)}) collective-permute-start(f32[48,768]{1,0:T(8,128)S(1)} %get-tuple-element.45.w_ref), channel_id=1, source_target_pairs={{0,1},{1,0},{2,3},{3,2},{4,5},{5,4},{6,7},{7,6},{8,9},{9,8},{10,11... | collective-permute-start | bytes 442376 | tf_op jit(solution)/shard_map/ppermute | solution.py:239
  31.3 11.6 %collective-permute-start.14 = (f32[48,768]{1,0:T(8,128)S(1)}, f32[48,768]{1,0:T(8,128)S(1)}, u32[]{:S(2)}, u32[]{:S(2)}) collective-permute-start(f32[48,768]{1,0:T(8,128)S(1)} %get-tuple-element.45.w_ref), channel_id=1, source_target_pairs={{1,2},{2,1},{3,4},{4,3},{5,6},{6,5},{7,0},{0,7},{9,10},{10,9},{11,... | collective-permute-start | bytes 442376 | tf_op jit(solution)/shard_map/ppermute | solution.py:239
  33.7 4.4 %collective-permute-start.15 = (f32[48,384]{1,0:T(8,128)S(1)}, f32[48,384]{1,0:T(8,128)S(1)}, u32[]{:S(2)}, u32[]{:S(2)}) collective-permute-start(f32[48,384]{1,0:T(8,128)S(1)} %get-tuple-element.46), channel_id=1, source_target_pairs={{0,16},{16,0},{1,17},{17,1},{2,18},{18,2},{3,19},{19,3},{4,20},{20... | collective-permute-start | bytes 221192 | tf_op jit(solution)/shard_map/ppermute | solution.py:239
  34.4 8.5 %collective-permute-start.16 = (f32[48,384]{1,0:T(8,128)S(1)}, f32[48,384]{1,0:T(8,128)S(1)}, u32[]{:S(2)}, u32[]{:S(2)}) collective-permute-start(f32[48,384]{1,0:T(8,128)S(1)} %get-tuple-element.46), channel_id=1, source_target_pairs={{0,17},{17,0},{1,18},{18,1},{2,19},{19,2},{3,20},{20,3},{4,21},{21... | collective-permute-start | bytes 221192 | tf_op jit(solution)/shard_map/ppermute | solution.py:239
  43.2 3.6 %collective-permute-start.17 = (f32[48,768]{1,0:T(8,128)S(1)}, f32[48,768]{1,0:T(8,128)S(1)}, u32[]{:S(2)}, u32[]{:S(2)}) collective-permute-start(f32[48,768]{1,0:T(8,128)S(1)} %get-tuple-element.47.w_ref), channel_id=1, source_target_pairs={{0,8},{8,0},{1,9},{9,1},{2,10},{10,2},{3,11},{11,3},{4,12},{12,4},... | collective-permute-start | bytes 442376 | tf_op jit(solution)/shard_map/ppermute | solution.py:239
  43.3 11.3 %collective-permute-start.18 = (f32[48,768]{1,0:T(8,128)S(1)}, f32[48,768]{1,0:T(8,128)S(1)}, u32[]{:S(2)}, u32[]{:S(2)}) collective-permute-start(f32[48,768]{1,0:T(8,128)S(1)} %get-tuple-element.47.w_ref), channel_id=1, source_target_pairs={{0,1},{1,0},{2,3},{3,2},{4,5},{5,4},{6,7},{7,6},{8,9},{9,8},{10,11... | collective-permute-start | bytes 442376 | tf_op jit(solution)/shard_map/ppermute | solution.py:239
  43.4 11.2 %collective-permute-start.19 = (f32[48,768]{1,0:T(8,128)S(1)}, f32[48,768]{1,0:T(8,128)S(1)}, u32[]{:S(2)}, u32[]{:S(2)}) collective-permute-start(f32[48,768]{1,0:T(8,128)S(1)} %get-tuple-element.47.w_ref), channel_id=1, source_target_pairs={{1,2},{2,1},{3,4},{4,3},{5,6},{6,5},{7,0},{0,7},{9,10},{10,9},{11,... | collective-permute-start | bytes 442376 | tf_op jit(solution)/shard_map/ppermute | solution.py:239
  45.8 4.4 %collective-permute-start.20 = (f32[48,384]{1,0:T(8,128)S(1)}, f32[48,384]{1,0:T(8,128)S(1)}, u32[]{:S(2)}, u32[]{:S(2)}) collective-permute-start(f32[48,384]{1,0:T(8,128)S(1)} %get-tuple-element.48), channel_id=1, source_target_pairs={{0,16},{16,0},{1,17},{17,1},{2,18},{18,2},{3,19},{19,3},{4,20},{20... | collective-permute-start | bytes 221192 | tf_op jit(solution)/shard_map/ppermute | solution.py:239
  46.6 7.9 %collective-permute-start.21 = (f32[48,384]{1,0:T(8,128)S(1)}, f32[48,384]{1,0:T(8,128)S(1)}, u32[]{:S(2)}, u32[]{:S(2)}) collective-permute-start(f32[48,384]{1,0:T(8,128)S(1)} %get-tuple-element.48), channel_id=1, source_target_pairs={{0,17},{17,0},{1,18},{18,1},{2,19},{19,2},{3,20},{20,3},{4,21},{21... | collective-permute-start | bytes 221192 | tf_op jit(solution)/shard_map/ppermute | solution.py:239
  54.9 1.3 %collective-permute-start.22 = (f32[48,384]{1,0:T(8,128)S(1)}, f32[48,384]{1,0:T(8,128)S(1)}, u32[]{:S(2)}, u32[]{:S(2)}) collective-permute-start(f32[48,384]{1,0:T(8,128)S(1)} %slice_select_fusion), channel_id=1, source_target_pairs={{0,8},{8,0},{1,9},{9,1},{2,10},{10,2},{3,11},{11,3},{4,12},{12,4},... | collective-permute-start | bytes 221192 | tf_op jit(solution)/shard_map/ppermute | solution.py:239

commit v3 on v2

--- a/solution.py
+++ b/solution.py
@@ -1,4 +1,5 @@
 import functools
+import math
 
 import jax
 import jax.numpy as jnp
@@ -7,6 +8,7 @@
 from jax.experimental import pallas as pl
 from jax.experimental.pallas import tpu as pltpu
 from jax.sharding import PartitionSpec as P
+
 
 TIME_STEP = 0.3
 HIGHEST = lax.Precision.HIGHEST
@@ -67,7 +69,7 @@
     return jnp.concatenate([value[:, half:], value[:, :half]], 1)
 
 
-def setup_kernel(slabs, links, chips, width, plan_ref, pick_ref, info_ref, ham_ref, coup_ref, base_ref, strength_ref, *outs):
+def setup_kernel(slabs, links, chips, width, plan_ref, pick_ref, info_ref, ham_ref, coup_ref, rates_ref, strength_ref, *outs):
     count = len(slabs)
     tables, (ham_out, right_out), (beta_ref, wide_ref, edge_ref) = outs[:count], outs[count : count + 2], outs[count + 2 :]
     tier, mode = lax.axis_index("tier"), lax.axis_index("mode")
@@ -88,7 +90,6 @@
 
     size = ham_ref.shape[0]
     half = size // 2
-    wide = coup_ref.shape[0]
     strong, weak = strength_ref[0:1, :], strength_ref[1:2, :]
     level = jnp.dot(pick_ref[...], info_ref[0], precision=HIGHEST, preferred_element_type=jnp.float32)
     ups = jnp.dot(pick_ref[...], info_ref[1], precision=HIGHEST, preferred_element_type=jnp.float32)
@@ -111,10 +112,12 @@
         col_w.append(jnp.where(straight, plus, -gap))
     row_w = jnp.concatenate(row_w, 0)
     drain = -plan_ref[3] * level
-    mine = base_ref[pl.ds(pl.multiple_of(core * half, 8), half), :]
+    turned = coup_ref[...].T
+    mine = jnp.where(core == 0, turned[:half], turned[half:])
     contract = (((1,), (1,)), ((), ()))
-    alpha = lax.dot_general(mine[:, :wide], row_w, contract, precision=HIGHEST, preferred_element_type=jnp.float32)
-    alpha += lax.dot_general(mine[:, wide:], drain, contract, precision=HIGHEST, preferred_element_type=jnp.float32)
+    alpha = lax.dot_general(mine, row_w, contract, precision=HIGHEST, preferred_element_type=jnp.float32)
+    every = jnp.broadcast_to(rates_ref[...], (half, rates_ref.shape[1]))
+    alpha += lax.dot_general(every, drain, contract, precision=HIGHEST, preferred_element_type=jnp.float32)
     beta_ref[...] = jnp.dot(jnp.concatenate(col_w, 0), coup_ref[...], precision=HIGHEST, preferred_element_type=jnp.float32)
     blocks = tables[0].shape[0]
     full_rows = 3 * blocks
@@ -151,7 +154,36 @@
         right_out[e * size : (e + 1) * size, e * size : (e + 1) * size] = ham
 
 
-def assemble_kernel(edges, keep_ref, got_ref, out_ref, *edge_refs):
+def split_kernel(count, *refs):
+    sources, (keep_ref, send_ref, facts_ref), copies = refs[:count], refs[count : count + 3], refs[count + 3 : 2 * count - 1]
+    raw_ref, lines_ref, rows_ref, sems = refs[2 * count - 1 :]
+    targets = [raw_ref] + [facts_ref.at[n] for n in range(3)] + list(copies)
+    moves = [pltpu.make_async_copy(a, b, sems.at[n]) for n, (a, b) in enumerate(zip(sources, targets))]
+    for move in moves:
+        move.start()
+    moves[0].wait()
+    core = lax.axis_index("tier") % 2
+    half, lanes = keep_ref.shape
+    size, (turns, groups, _) = 2 * half, lines_ref.shape
+    lines = size * turns // 128
+    for s in range(raw_ref.shape[0]):
+        for part in (0, 1):
+            flat = [raw_ref[s, pl.ds(2 * p + part, groups, stride=2 * lines), :] for p in range(lines)]
+            flat = jnp.concatenate(flat, 1)
+            block = (2 * s + part) * size
+            for q in range(turns):
+                lines_ref[q, :, block : block + size] = flat[:, q * size : (q + 1) * size]
+    for v in range(lanes // 128):
+        at = slice(128 * v, 128 * v + 128)
+        for q in range(turns):
+            rows_ref[v, pl.ds(q, groups, stride=turns), :] = lines_ref[q, :, at]
+        keep_ref[:, at] = rows_ref[v, pl.ds(pl.multiple_of(core * half, 8), half), :]
+        send_ref[:, at] = rows_ref[v, pl.ds(pl.multiple_of((1 - core) * half, 8), half), :]
+    for move in moves[1:]:
+        move.wait()
+
+
+def assemble_kernel(edges, keep_ref, got_ref, facts_ref, other_ref, out_ref, info_ref, *edge_refs):
     tier = lax.axis_index("tier")
     first = ((tier % 2) ^ ((tier // 2) % 2)) == 0
     lanes = keep_ref.shape[1]
@@ -161,41 +193,73 @@
     out_ref[:, lanes:] = halves[1]
     for n, place in enumerate(edges):
         edge_refs[n][...] = halves[place]
-
-
-def own_kernel(step, width, w_ref, other_ref, start_ref, ham_ref, right_ref, table_ref, out_ref, comm_ref):
+    slots = facts_ref.shape[1]
+    for n in range(3):
+        mine, other = facts_ref[n].astype(jnp.float32), other_ref[n].astype(jnp.float32)
+        info_ref[n, :slots, :] = jnp.where(first, mine, other)
+        info_ref[n, slots:, :] = jnp.where(first, other, mine)
+
+
+def finish_kernel(keep_ref, got_ref, out_ref, rows_ref, lines_ref):
+    upper = lax.axis_index("tier") % 2 == 0
+    half = keep_ref.shape[0]
+    size, (groups, length) = 2 * half, lines_ref.shape[1:]
+    turns, lines = length // size, length // 128
+    planes = rows_ref.shape[0]
+    for v in range(planes):
+        at = slice(128 * v, 128 * v + 128)
+        keep, got = keep_ref[:, at], got_ref[:, at]
+        rows_ref[v, :half] = jnp.where(upper, keep, got)
+        rows_ref[v, half:] = jnp.where(upper, got, keep)
+    rows = [[rows_ref[v, pl.ds(q, groups, stride=turns), :] for v in range(planes)] for q in range(turns)]
+    rows = [jnp.concatenate(r, 1) for r in rows]
+    for s in range(out_ref.shape[0]):
+        for part in (0, 1):
+            block = 2 * s + part
+            for q in range(turns):
+                lines_ref[block, :, q * size : (q + 1) * size] = rows[q][:, block * size : (block + 1) * size]
+            for p in range(lines):
+                out_ref[s, pl.ds(2 * p + part, groups, stride=2 * lines), :] = lines_ref[block, :, 128 * p : 128 * (p + 1)]
+
+
+def own_kernel(step, width, w_ref, start_ref, right_ref, table_ref, out_ref, right_out):
     rows, lanes = w_ref.shape
     half = lanes // 2
-    w = w_ref[...]
-    both = jnp.concatenate([w, other_ref[...]], 0)
-    left = jnp.dot(ham_ref[...], both, precision=HIGHEST, preferred_element_type=jnp.float32)
-    stacked = jnp.concatenate([w[:, :half], w[:, half:]], 0)
+    stacked = jnp.concatenate([w_ref[:, :half], w_ref[:, half:]], 0)
     right = jnp.dot(stacked, right_ref[...], precision=HIGHEST, preferred_element_type=jnp.float32)
-    comm_ref[:, :half] = left[:, :half] - right[:rows]
-    comm_ref[:, half:] = left[:, half:] - right[rows:]
+    right_out[:, :half] = right[:rows]
+    right_out[:, half:] = right[rows:]
     blocks = table_ref.shape[0]
+    for at in range(0, rows, 8):
+        part = pl.ds(at, 8)
+        value = w_ref[part, :]
+        total = None
+        for k in range(blocks // 2):
+            near, far = table_ref[k, part, :] * value, table_ref[k + blocks // 2, part, :] * value
+            piece = turned(near + swapped(far), k, width)
+            total = piece if total is None else total + piece
+        out_ref[part, :] = start_ref[part, :] + step * total
+
+
+def left_kernel(step, width, w_ref, other_ref, ham_ref, part_ref, right_ref, out_ref, comm_ref):
+    rows, lanes = w_ref.shape
+    both = jnp.concatenate([w_ref[...], other_ref[...]], 0)
+    comm_ref[...] = jnp.dot(ham_ref[...], both, precision=HIGHEST, preferred_element_type=jnp.float32)
     odd = (lax.broadcasted_iota(jnp.int32, (8, lanes), 1) // width) % 2 == 1
     for at in range(0, rows, 8):
         part = pl.ds(at, 8)
-        value, comm = w_ref[part, :], comm_ref[part, :]
-        total = None
-        for k in range(blocks // 2):
-            near = table_ref[k, part, :] * value
-            far = table_ref[k + blocks // 2, part, :] * value
-            if k == 1:
-                near += jnp.where(odd, 0.0, -comm)
-            if k + blocks // 2 == blocks - 1:
-                far += jnp.where(odd, comm, 0.0)
-            piece = turned(near + swapped(far), k, width)
-            total = piece if total is None else total + piece
-        out_ref[part, :] = start_ref[part, :] + step * total
-
-
-def link_kernel(step, width, edges, *refs):
+        comm = step * (comm_ref[part, :] - right_ref[part, :])
+        real = pltpu.roll(jnp.where(odd, comm, 0.0), lanes - width, 1)
+        imag = pltpu.roll(jnp.where(odd, 0.0, comm), width, 1)
+        out_ref[part, :] = part_ref[part, :] + (real - imag)
+
+
+def link_kernel(step, width, edges, last, *refs):
     part_ref, x_ref, z_ref, x_table, z_table = refs[:5]
     edge_refs = refs[5 : 5 + 4 * len(edges)]
-    out_ref = refs[5 + 4 * len(edges)]
-    edge_out = refs[6 + 4 * len(edges) :]
+    outs = refs[5 + 4 * len(edges) :]
+    tier = lax.axis_index("tier")
+    first = ((tier % 2) ^ ((tier // 2) % 2)) == 0
     rows, lanes = part_ref.shape
     half = lanes // 2
     blocks = x_table.shape[0]
@@ -217,10 +281,14 @@
                 piece = flat_table[k, part, :] * a + slant_table[k, part, :] * b
                 halves[place] = halves[place] + turned(piece, k, width)
         new = [part_ref[part, :half] + step * halves[0], part_ref[part, half:] + step * halves[1]]
-        out_ref[part, :half] = new[0]
-        out_ref[part, half:] = new[1]
-        for n, place in enumerate(edges[: len(edge_out)]):
-            edge_out[n][part, :] = new[place]
+        if last:
+            outs[0][part, :] = jnp.where(first, new[0], new[1])
+            outs[1][part, :] = jnp.where(first, new[1], new[0])
+            continue
+        outs[0][part, :half] = new[0]
+        outs[0][part, half:] = new[1]
+        for n, place in enumerate(edges):
+            outs[1 + n][part, :] = new[place]
 
 
 VMEM = pl.BlockSpec(memory_space=pltpu.VMEM)
@@ -231,50 +299,61 @@
     core_route, mode_routes, flat_routes, slant_routes = routes(tiers, modes)
     slots, size = ados.shape[2], hamiltonian.shape[0]
     half, lanes = size // 2, slots * 2 * size
-    tier, mode = lax.axis_index("tier"), lax.axis_index("mode")
-    core, chip = tier % 2, tier // 2
-    place = core ^ (chip % 2)
 
     def send(value, route):
         return lax.ppermute(value, AXES, route)
 
-    facts = jnp.stack([a.reshape(a.shape[2:]) for a in (occupancy, up_index, down_index)])
-    other_facts = send(facts, core_route)
-    own = ados.reshape(slots * 2, size, size).transpose(1, 0, 2).reshape(size, lanes)
-    keep = lax.dynamic_slice(own, (core * half, 0), (half, lanes))
-    got = send(lax.dynamic_slice(own, ((1 - core) * half, 0), (half, lanes)), core_route)
-    first = place == 0
+    turns = 128 // math.gcd(size, 128)
+    groups, count = size // turns, size * size // 128
+    raw = ados.reshape(slots, 2, count, 128).transpose(0, 2, 1, 3).reshape(slots, 2 * count, 128)
+    edge = jax.ShapeDtypeStruct((half, lanes), jnp.float32)
+    full = jax.ShapeDtypeStruct((half, 2 * lanes), jnp.float32)
     links = [p for p in (0, 1) if flat_routes[p]]
     edges = tuple(1 - p for p in links)
-    full = jax.ShapeDtypeStruct((half, 2 * lanes), jnp.float32)
-    edge = jax.ShapeDtypeStruct((half, lanes), jnp.float32)
-    start, *brink = pl.pallas_call(
+    bath = couplings.shape[0]
+    slabs = setup_plan(slots, edges)
+    plan = np.concatenate(slabs, 0)
+    pick = np.eye(2 * slots, dtype=np.float32)[plan[:, 0].astype(np.int32)]
+    plan = np.broadcast_to(plan.T[1:, :, None], (4, plan.shape[0], bath)).copy()
+    index = [a.reshape(slots, bath) for a in (occupancy, up_index, down_index)]
+    small = [hamiltonian, couplings, rates.reshape(1, bath), strength, plan, pick]
+    count_in = 4 + len(small)
+    keep, away, facts, *small = pl.pallas_call(
+        functools.partial(split_kernel, count_in),
+        out_shape=[edge, edge, jax.ShapeDtypeStruct((3, slots, bath), jnp.int32)]
+        + [jax.ShapeDtypeStruct(a.shape, jnp.float32) for a in small],
+        in_specs=[pl.BlockSpec(memory_space=pltpu.HBM)] * count_in,
+        out_specs=[VMEM] * (3 + len(small)),
+        scratch_shapes=[
+            pltpu.VMEM(raw.shape, jnp.float32),
+            pltpu.VMEM((turns, groups, lanes), jnp.float32),
+            pltpu.VMEM((lanes // 128, size, 128), jnp.float32),
+            pltpu.SemaphoreType.DMA((count_in,)),
+        ],
+        compiler_params=GRANT,
+        name="split",
+    )(*[pltpu.with_memory_space_constraint(jnp.asarray(a), pltpu.HBM) for a in (raw, *index, *small)])
+    other_facts = send(facts, core_route)
+    got = send(away, core_route)
+    start, info, *brink = pl.pallas_call(
         functools.partial(assemble_kernel, edges),
-        out_shape=[full] + [edge] * len(links),
-        in_specs=[VMEM] * 2,
-        out_specs=[VMEM] * (1 + len(links)),
+        out_shape=[full, jax.ShapeDtypeStruct((3, 2 * slots, bath), jnp.float32)] + [edge] * len(links),
+        in_specs=[VMEM] * 4,
+        out_specs=[VMEM] * (2 + len(links)),
         compiler_params=GRANT,
         name="assemble",
-    )(keep, got)
-
-    late = (start, facts, other_facts, hamiltonian, couplings, rates, strength)
-    start, facts, other_facts, hamiltonian, couplings, rates, strength = lax.optimization_barrier(late)
-    info = jnp.concatenate([jnp.where(first, facts, other_facts), jnp.where(first, other_facts, facts)], 1)
-    info = info.astype(jnp.float32)
-    slabs = setup_plan(slots, edges)
-    plan = np.concatenate(slabs, 0)
-    bath = couplings.shape[0]
-    pick = np.eye(2 * slots, dtype=np.float32)[plan[:, 0].astype(np.int32)]
-    plan = np.broadcast_to(plan.T[1:, :, None], (4, plan.shape[0], bath)).copy()
-    base = jnp.concatenate([couplings.T, jnp.broadcast_to(rates[None, :], (size, bath))], 1)
+    )(keep, got, facts, other_facts)
+
+    start, info, small = lax.optimization_barrier((start, info, small))
+    hamiltonian, couplings, rates, strength, plan, pick = small
     blocks = 4 * slots
     big = jax.ShapeDtypeStruct((blocks, half, 2 * lanes), jnp.float32)
-    small = jax.ShapeDtypeStruct((blocks // 2, half, lanes), jnp.float32)
+    narrow = jax.ShapeDtypeStruct((blocks // 2, half, lanes), jnp.float32)
     edge_count = 2 * len(links)
     *tables, ham, right = pl.pallas_call(
         functools.partial(setup_kernel, slabs, links, tiers // 2, size),
         out_shape=[big] * 3
-        + [small] * edge_count
+        + [narrow] * edge_count
         + [jax.ShapeDtypeStruct((half, size), jnp.float32), jax.ShapeDtypeStruct((lanes, lanes), jnp.float32)],
         in_specs=[VMEM] * 7,
         out_specs=[VMEM] * (5 + edge_count),
@@ -285,7 +364,7 @@
         ],
         compiler_params=GRANT,
         name="setup",
-    )(plan, pick, info, hamiltonian, couplings, base, strength)
+    )(plan, pick, info, hamiltonian, couplings, rates, strength)
 
     w = start
     for stage in (4, 3, 2, 1):
@@ -295,32 +374,45 @@
         z = send(w, mode_routes[1])
         x = send(w, mode_routes[0])
         other = send(w, core_route)
+        part, product = pl.pallas_call(
+            functools.partial(own_kernel, step, size),
+            out_shape=[full, full],
+            in_specs=[VMEM] * 4,
+            out_specs=[VMEM] * 2,
+            compiler_params=GRANT,
+            name="own_part",
+        )(w, start, right, tables[0])
         part = pl.pallas_call(
-            functools.partial(own_kernel, step, size),
+            functools.partial(left_kernel, step, size),
             out_shape=full,
-            in_specs=[VMEM] * 6,
+            in_specs=[VMEM] * 5,
             out_specs=VMEM,
             scratch_shapes=[pltpu.VMEM((half, 2 * lanes), jnp.float32)],
             compiler_params=GRANT,
-            name="own_part",
-        )(w, other, start, ham, right, tables[0])
+            name="left_part",
+        )(w, other, ham, part, product)
         extra = [a for n in range(len(links)) for a in (flat[n], slant[n], *tables[3 + 2 * n : 5 + 2 * n])]
-        count = len(links) if stage > 1 else 0
-        result = pl.pallas_call(
-            functools.partial(link_kernel, step, size, edges),
-            out_shape=[full] + [edge] * count,
+        last = stage == 1
+        shapes = [edge] * 2 if last else [full] + [edge] * len(links)
+        w, *brink = pl.pallas_call(
+            functools.partial(link_kernel, step, size, edges, last),
+            out_shape=shapes,
             in_specs=[VMEM] * (5 + len(extra)),
-            out_specs=[VMEM] * (1 + count),
+            out_specs=[VMEM] * len(shapes),
             compiler_params=GRANT,
             name="link_part",
         )(part, x, z, tables[1], tables[2], *extra)
-        w, brink = result[0], result[1:]
-
-    low, high = w[:, :lanes], w[:, lanes:]
-    keep = jnp.where(first, low, high)
-    got = send(jnp.where(first, high, low), core_route)
-    whole = jnp.concatenate([jnp.where(core == 0, keep, got), jnp.where(core == 0, got, keep)], 0)
-    return whole.reshape(size, slots * 2, size).transpose(1, 0, 2).reshape(ados.shape)
+
+    out = pl.pallas_call(
+        finish_kernel,
+        out_shape=jax.ShapeDtypeStruct(raw.shape, jnp.float32),
+        in_specs=[VMEM] * 2,
+        out_specs=VMEM,
+        scratch_shapes=[pltpu.VMEM((lanes // 128, size, 128), jnp.float32), pltpu.VMEM((2 * slots, groups, turns * size), jnp.float32)],
+        compiler_params=GRANT,
+        name="finish",
+    )(w, send(brink[0], core_route))
+    return out.reshape(slots, count, 2, 128).transpose(0, 2, 1, 3).reshape(ados.shape)
 
 
 def solution(mesh):

time: 57.5 us -> 56.8 us (0.988)
  local copies, waits for them, and re-layouts: 2.77 us -> 0 us
  Pallas kernels: 7.79 us -> 10.4 us
    reshape x5 -> x0, local copies, waits for them, and re-layouts: 2.54 us -> none  [the longest x3 1.48 us: shards(): ados.reshape(slots * 2, size, size).transpose(1, 0, 2).reshape(size, lanes)]
    pallas_call x8 -> x14, Pallas kernels: 4.3 us -> 6.8 us  [the longest x4 2.01 us: shards(): pl.pallas_call(functools.partial(own_kernel, step, size), out_shape=[full...]
  transfers between devices with their start and end apart: 23 -> 23, of which waited for: 10 -> 9; matrix products, arithmetic and copies ran while one was open for 0% -> 0% of each run, Pallas kernels for 11% -> 12%
where the time goes in v3:
time: 56.8 us; the launch traced here: 56.7 us
  waiting for transfers between devices  25.3 us (45%)
  starting transfers between devices  20.8 us (37%)
  Pallas kernels  10.4 us (18%)
    ppermute x23, waiting for transfers between devices, send(): return lax.ppermute(value, AXES, route)  25.3 us
    ppermute x23, starting transfers between devices, send(): return lax.ppermute(value, AXES, route)  20.8 us
    pallas_call x1, Pallas kernels, shards(): pl.pallas_call(functools.partial(setup_kernel, slabs, links, tiers // 2,...  3.53 us
    pallas_call x4, Pallas kernels, shards(): pl.pallas_call(functools.partial(own_kernel, step, size), out_shape=[full...  2.01 us
    pallas_call x4, Pallas kernels, shards(): pl.pallas_call(functools.partial(left_kernel, step, size), out_shape=full...  1.49 us
    pallas_call x1, Pallas kernels, shards(): pl.pallas_call(functools.partial(split_kernel, count_in), out_shape=[edge...  1.32 us
    pallas_call x4, Pallas kernels, shards(): pl.pallas_call(functools.partial(link_kernel, step, size, edges, last), o...  1.15 us
  transfers between devices with their start and end apart: 23, of which 9 were waited for; matrix products, arithmetic and copies ran while one was open for 0% of the time, Pallas kernels for 12%

profile of v3, /device:TPU:0, one launch (start us, length us, event | category | flops | bytes accessed | tf_op | source)
XLA Modules:
  0.0 56.7 jit_solution(8641892774617791478)
XLA Ops:
  0.0 1.3 %split.1 = (f32[48,384]{1,0:T(8,128)S(1)}, f32[48,384]{1,0:T(8,128)S(1)}, s32[3,2,16]{2,1,0:T(2,128)S(1)}, f32[96,96]{1,0:T(8,128)S(1)}, f32[16,96]{1,0:T(8,128)...) custom-call(f32[2,144,128]{2,1,0:T(8,128)} %bitcast.14, ...), custom_call_target="tpu_custom_call" | custom-call | tf_op jit(solution)/shard_map/split/pallas_call | solution.py:321
  1.3 0.6 collective-permute-start
  2.0 1.1 %collective-permute-done.1.other_ref = s32[3,2,16]{2,1,0:T(2,128)S(1)} collective-permute-done((s32[3,2,16]{2,1,0:T(2,128)S(1)}, s32[3,2,16]{2,1,0:T(2,128)S(1)}, u32[]{:S(2)}, u32[]{:S(2)}) %collective-permute-start.1) | collective-permute-done | bytes 416 | tf_op jit(solution)/shard_map/ppermute | solution.py:304
  3.3 2.8 %collective-permute-start.3 = (f32[48,768]{1,0:T(8,128)S(1)}, f32[48,768]{1,0:T(8,128)S(1)}, u32[]{:S(2)}, u32[]{:S(2)}) collective-permute-start(f32[48,768]{1,0:T(8,128)S(1)} %get-tuple-element.59.w_ref.start_ref), channel_id=1, source_target_pairs={{0,1},{1,0},{2,3},{3,2},{4,5},{5,4},{6,7},{7,6},{8,9},{9,8},{10,11... | collective-permute-start | bytes 442376 | tf_op jit(solution)/shard_map/ppermute | solution.py:304
  6.2 3.6 %collective-permute-start.4 = (f32[48,768]{1,0:T(8,128)S(1)}, f32[48,768]{1,0:T(8,128)S(1)}, u32[]{:S(2)}, u32[]{:S(2)}) collective-permute-start(f32[48,768]{1,0:T(8,128)S(1)} %get-tuple-element.59.w_ref.start_ref), channel_id=1, source_target_pairs={{1,2},{2,1},{3,4},{4,3},{5,6},{6,5},{7,0},{0,7},{9,10},{10,9},{11,... | collective-permute-start | bytes 442376 | tf_op jit(solution)/shard_map/ppermute | solution.py:304
  9.7 1.5 %collective-permute-start.5 = (f32[48,384]{1,0:T(8,128)S(1)}, f32[48,384]{1,0:T(8,128)S(1)}, u32[]{:S(2)}, u32[]{:S(2)}) collective-permute-start(f32[48,384]{1,0:T(8,128)S(1)} %get-tuple-element.74), channel_id=1, source_target_pairs={{0,16},{16,0},{1,17},{17,1},{2,18},{18,2},{3,19},{19,3},{4,20},{20... | collective-permute-start | bytes 221192 | tf_op jit(solution)/shard_map/ppermute | solution.py:304
  11.2 3.5 %setup.1 = (f32[8,48,768]{2,1,0:T(8,128)S(1)}, f32[8,48,768]{2,1,0:T(8,128)S(1)}, f32[8,48,768]{2,1,0:T(8,128)S(1)}, f32[4,48,384]{2,1,0:T(8,128)S(1)}, f32[4,48...) custom-call(f32[4,224,16]{2,1,0:T(8,128)S(1)} %get-tuple-element.60.plan_ref, ...), custom_call_target="tpu_custom_call" | custom-call | tf_op jit(solution)/shard_map/setup/pallas_call | solution.py:353
  14.8 0.5 own_part.4
  15.3 0.4 left_part.4.refs_0_
  15.7 1.3 %collective-permute-done.6.refs_6_ = f32[48,384]{1,0:T(8,128)S(1)} collective-permute-done((f32[48,384]{1,0:T(8,128)S(1)}, f32[48,384]{1,0:T(8,128)S(1)}, u32[]{:S(2)}, u32[]{:S(2)}) %collective-permute-start.6) | collective-permute-done | bytes 73760 | tf_op jit(solution)/shard_map/ppermute | solution.py:304
  17.5 4.3 %collective-permute-start.9 = (f32[48,768]{1,0:T(8,128)S(1)}, f32[48,768]{1,0:T(8,128)S(1)}, u32[]{:S(2)}, u32[]{:S(2)}) collective-permute-start(f32[48,768]{1,0:T(8,128)S(1)} %get-tuple-element.77.w_ref), channel_id=1, source_target_pairs={{1,2},{2,1},{3,4},{4,3},{5,6},{6,5},{7,0},{0,7},{9,10},{10,9},{11,... | collective-permute-start | bytes 442376 | tf_op jit(solution)/shard_map/ppermute | solution.py:304
  22.1 0.5 own_part.5
  22.6 0.4 left_part.5.refs_0_
  22.9 3.2 %collective-permute-done.10.refs_5_ = f32[48,384]{1,0:T(8,128)S(1)} collective-permute-done((f32[48,384]{1,0:T(8,128)S(1)}, f32[48,384]{1,0:T(8,128)S(1)}, u32[]{:S(2)}, u32[]{:S(2)}) %collective-permute-start.10) | collective-permute-done | bytes 73760 | tf_op jit(solution)/shard_map/ppermute | solution.py:304
  26.2 4.3 %collective-permute-done.11.refs_6_ = f32[48,384]{1,0:T(8,128)S(1)} collective-permute-done((f32[48,384]{1,0:T(8,128)S(1)}, f32[48,384]{1,0:T(8,128)S(1)}, u32[]{:S(2)}, u32[]{:S(2)}) %collective-permute-start.11) | collective-permute-done | bytes 73760 | tf_op jit(solution)/shard_map/ppermute | solution.py:304
  30.5 0.3 link_part.5
  31.0 2.5 %collective-permute-start.14 = (f32[48,768]{1,0:T(8,128)S(1)}, f32[48,768]{1,0:T(8,128)S(1)}, u32[]{:S(2)}, u32[]{:S(2)}) collective-permute-start(f32[48,768]{1,0:T(8,128)S(1)} %get-tuple-element.81.w_ref), channel_id=1, source_target_pairs={{1,2},{2,1},{3,4},{4,3},{5,6},{6,5},{7,0},{0,7},{9,10},{10,9},{11,... | collective-permute-start | bytes 442376 | tf_op jit(solution)/shard_map/ppermute | solution.py:304
  33.4 0.6 %collective-permute-start.15 = (f32[48,384]{1,0:T(8,128)S(1)}, f32[48,384]{1,0:T(8,128)S(1)}, u32[]{:S(2)}, u32[]{:S(2)}) collective-permute-start(f32[48,384]{1,0:T(8,128)S(1)} %get-tuple-element.84), channel_id=1, source_target_pairs={{0,16},{16,0},{1,17},{17,1},{2,18},{18,2},{3,19},{19,3},{4,20},{20... | collective-permute-start | bytes 221192 | tf_op jit(solution)/shard_map/ppermute | solution.py:304
  34.1 0.4 collective-permute-start.16
  34.4 0.5 own_part.6
  35.0 0.4 left_part.6.refs_0_
  35.3 2.5 %collective-permute-done.15.refs_5_ = f32[48,384]{1,0:T(8,128)S(1)} collective-permute-done((f32[48,384]{1,0:T(8,128)S(1)}, f32[48,384]{1,0:T(8,128)S(1)}, u32[]{:S(2)}, u32[]{:S(2)}) %collective-permute-start.15) | collective-permute-done | bytes 73760 | tf_op jit(solution)/shard_map/ppermute | solution.py:304
  37.8 4.7 %collective-permute-done.16.refs_6_ = f32[48,384]{1,0:T(8,128)S(1)} collective-permute-done((f32[48,384]{1,0:T(8,128)S(1)}, f32[48,384]{1,0:T(8,128)S(1)}, u32[]{:S(2)}, u32[]{:S(2)}) %collective-permute-start.16) | collective-permute-done | bytes 73760 | tf_op jit(solution)/shard_map/ppermute | solution.py:304
  42.6 0.3 link_part.6
  43.0 2.5 %collective-permute-start.19 = (f32[48,768]{1,0:T(8,128)S(1)}, f32[48,768]{1,0:T(8,128)S(1)}, u32[]{:S(2)}, u32[]{:S(2)}) collective-permute-start(f32[48,768]{1,0:T(8,128)S(1)} %get-tuple-element.85.w_ref), channel_id=1, source_target_pairs={{1,2},{2,1},{3,4},{4,3},{5,6},{6,5},{7,0},{0,7},{9,10},{10,9},{11,... | collective-permute-start | bytes 442376 | tf_op jit(solution)/shard_map/ppermute | solution.py:304
  45.5 0.8 %collective-permute-start.20 = (f32[48,384]{1,0:T(8,128)S(1)}, f32[48,384]{1,0:T(8,128)S(1)}, u32[]{:S(2)}, u32[]{:S(2)}) collective-permute-start(f32[48,384]{1,0:T(8,128)S(1)} %get-tuple-element.88), channel_id=1, source_target_pairs={{0,16},{16,0},{1,17},{17,1},{2,18},{18,2},{3,19},{19,3},{4,20},{20... | collective-permute-start | bytes 221192 | tf_op jit(solution)/shard_map/ppermute | solution.py:304
  46.5 0.5 own_part.7
  47.0 0.4 left_part.7.refs_0_
  47.4 2.4 %collective-permute-done.20.refs_5_ = f32[48,384]{1,0:T(8,128)S(1)} collective-permute-done((f32[48,384]{1,0:T(8,128)S(1)}, f32[48,384]{1,0:T(8,128)S(1)}, u32[]{:S(2)}, u32[]{:S(2)}) %collective-permute-start.20) | collective-permute-done | bytes 73760 | tf_op jit(solution)/shard_map/ppermute | solution.py:304
  49.8 4.4 %collective-permute-done.21.refs_6_ = f32[48,384]{1,0:T(8,128)S(1)} collective-permute-done((f32[48,384]{1,0:T(8,128)S(1)}, f32[48,384]{1,0:T(8,128)S(1)}, u32[]{:S(2)}, u32[]{:S(2)}) %collective-permute-start.21) | collective-permute-done | bytes 73760 | tf_op jit(solution)/shard_map/ppermute | solution.py:304
  54.6 1.3 %collective-permute-done.22.got_ref = f32[48,384]{1,0:T(8,128)S(1)} collective-permute-done((f32[48,384]{1,0:T(8,128)S(1)}, f32[48,384]{1,0:T(8,128)S(1)}, u32[]{:S(2)}, u32[]{:S(2)}) %collective-permute-start.22) | collective-permute-done | bytes 73760 | tf_op jit(solution)/shard_map/ppermute | solution.py:304
  55.8 0.8 %finish.1 = f32[2,144,128]{2,1,0:T(8,128)} custom-call(f32[48,384]{1,0:T(8,128)S(1)} %get-tuple-element.89.keep_ref, f32[48,384]{1,0:T(8,128)S(1)} %collective-permute-done.22.got_ref), custom_call_target="tpu_custom_call" | custom-call | tf_op jit(solution)/shard_map/finish/pallas_call | solution.py:406
  (30 shorter events, 2.0 us)
Async XLA Ops:
  1.3 1.7 %collective-permute-start = (f32[48,384]{1,0:T(8,128)S(1)}, f32[48,384]{1,0:T(8,128)S(1)}, u32[]{:S(2)}, u32[]{:S(2)}) collective-permute-start(f32[48,384]{1,0:T(8,128)S(1)} %get-tuple-element.49), channel_id=1, source_target_pairs={{0,8},{8,0},{1,9},{9,1},{2,10},{10,2},{3,11},{11,3},{4,12},{12,4},... | collective-permute-start | bytes 221192 | tf_op jit(solution)/shard_map/ppermute | solution.py:304
  1.9 1.2 %collective-permute-start.1 = (s32[3,2,16]{2,1,0:T(2,128)S(1)}, s32[3,2,16]{2,1,0:T(2,128)S(1)}, u32[]{:S(2)}, u32[]{:S(2)}) collective-permute-start(s32[3,2,16]{2,1,0:T(2,128)S(1)} %get-tuple-element.50.facts_ref), channel_id=1, source_target_pairs={{0,8},{8,0},{1,9},{9,1},{2,10},{10,2},{3,11},{11,3},{4,12},{12,4},... | collective-permute-start | bytes 1160 | tf_op jit(solution)/shard_map/ppermute | solution.py:304
  3.1 12.2 %collective-permute-start.2 = (f32[48,768]{1,0:T(8,128)S(1)}, f32[48,768]{1,0:T(8,128)S(1)}, u32[]{:S(2)}, u32[]{:S(2)}) collective-permute-start(f32[48,768]{1,0:T(8,128)S(1)} %get-tuple-element.59.w_ref.start_ref), channel_id=1, source_target_pairs={{0,8},{8,0},{1,9},{9,1},{2,10},{10,2},{3,11},{11,3},{4,12},{12,4},... | collective-permute-start | bytes 442376 | tf_op jit(solution)/shard_map/ppermute | solution.py:304
  3.3 13.7 %collective-permute-start.3 = (f32[48,768]{1,0:T(8,128)S(1)}, f32[48,768]{1,0:T(8,128)S(1)}, u32[]{:S(2)}, u32[]{:S(2)}) collective-permute-start(f32[48,768]{1,0:T(8,128)S(1)} %get-tuple-element.59.w_ref.start_ref), channel_id=1, source_target_pairs={{0,1},{1,0},{2,3},{3,2},{4,5},{5,4},{6,7},{7,6},{8,9},{9,8},{10,11... | collective-permute-start | bytes 442376 | tf_op jit(solution)/shard_map/ppermute | solution.py:304
  6.2 10.9 %collective-permute-start.4 = (f32[48,768]{1,0:T(8,128)S(1)}, f32[48,768]{1,0:T(8,128)S(1)}, u32[]{:S(2)}, u32[]{:S(2)}) collective-permute-start(f32[48,768]{1,0:T(8,128)S(1)} %get-tuple-element.59.w_ref.start_ref), channel_id=1, source_target_pairs={{1,2},{2,1},{3,4},{4,3},{5,6},{6,5},{7,0},{0,7},{9,10},{10,9},{11,... | collective-permute-start | bytes 442376 | tf_op jit(solution)/shard_map/ppermute | solution.py:304
  9.7 6.0 %collective-permute-start.5 = (f32[48,384]{1,0:T(8,128)S(1)}, f32[48,384]{1,0:T(8,128)S(1)}, u32[]{:S(2)}, u32[]{:S(2)}) collective-permute-start(f32[48,384]{1,0:T(8,128)S(1)} %get-tuple-element.74), channel_id=1, source_target_pairs={{0,16},{16,0},{1,17},{17,1},{2,18},{18,2},{3,19},{19,3},{4,20},{20... | collective-permute-start | bytes 221192 | tf_op jit(solution)/shard_map/ppermute | solution.py:304
  11.2 5.8 %collective-permute-start.6 = (f32[48,384]{1,0:T(8,128)S(1)}, f32[48,384]{1,0:T(8,128)S(1)}, u32[]{:S(2)}, u32[]{:S(2)}) collective-permute-start(f32[48,384]{1,0:T(8,128)S(1)} %get-tuple-element.74), channel_id=1, source_target_pairs={{0,17},{17,0},{1,18},{18,1},{2,19},{19,2},{3,20},{20,3},{4,21},{21... | collective-permute-start | bytes 221192 | tf_op jit(solution)/shard_map/ppermute | solution.py:304
  17.3 5.2 %collective-permute-start.7 = (f32[48,768]{1,0:T(8,128)S(1)}, f32[48,768]{1,0:T(8,128)S(1)}, u32[]{:S(2)}, u32[]{:S(2)}) collective-permute-start(f32[48,768]{1,0:T(8,128)S(1)} %get-tuple-element.77.w_ref), channel_id=1, source_target_pairs={{0,8},{8,0},{1,9},{9,1},{2,10},{10,2},{3,11},{11,3},{4,12},{12,4},... | collective-permute-start | bytes 442376 | tf_op jit(solution)/shard_map/ppermute | solution.py:304
  17.4 13.1 %collective-permute-start.8 = (f32[48,768]{1,0:T(8,128)S(1)}, f32[48,768]{1,0:T(8,128)S(1)}, u32[]{:S(2)}, u32[]{:S(2)}) collective-permute-start(f32[48,768]{1,0:T(8,128)S(1)} %get-tuple-element.77.w_ref), channel_id=1, source_target_pairs={{0,1},{1,0},{2,3},{3,2},{4,5},{5,4},{6,7},{7,6},{8,9},{9,8},{10,11... | collective-permute-start | bytes 442376 | tf_op jit(solution)/shard_map/ppermute | solution.py:304
  17.5 13.0 %collective-permute-start.9 = (f32[48,768]{1,0:T(8,128)S(1)}, f32[48,768]{1,0:T(8,128)S(1)}, u32[]{:S(2)}, u32[]{:S(2)}) collective-permute-start(f32[48,768]{1,0:T(8,128)S(1)} %get-tuple-element.77.w_ref), channel_id=1, source_target_pairs={{1,2},{2,1},{3,4},{4,3},{5,6},{6,5},{7,0},{0,7},{9,10},{10,9},{11,... | collective-permute-start | bytes 442376 | tf_op jit(solution)/shard_map/ppermute | solution.py:304
  21.8 4.4 %collective-permute-start.10 = (f32[48,384]{1,0:T(8,128)S(1)}, f32[48,384]{1,0:T(8,128)S(1)}, u32[]{:S(2)}, u32[]{:S(2)}) collective-permute-start(f32[48,384]{1,0:T(8,128)S(1)} %get-tuple-element.80), channel_id=1, source_target_pairs={{0,16},{16,0},{1,17},{17,1},{2,18},{18,2},{3,19},{19,3},{4,20},{20... | collective-permute-start | bytes 221192 | tf_op jit(solution)/shard_map/ppermute | solution.py:304
  22.0 8.5 %collective-permute-start.11 = (f32[48,384]{1,0:T(8,128)S(1)}, f32[48,384]{1,0:T(8,128)S(1)}, u32[]{:S(2)}, u32[]{:S(2)}) collective-permute-start(f32[48,384]{1,0:T(8,128)S(1)} %get-tuple-element.80), channel_id=1, source_target_pairs={{0,17},{17,0},{1,18},{18,1},{2,19},{19,2},{3,20},{20,3},{4,21},{21... | collective-permute-start | bytes 221192 | tf_op jit(solution)/shard_map/ppermute | solution.py:304
  30.8 4.1 %collective-permute-start.12 = (f32[48,768]{1,0:T(8,128)S(1)}, f32[48,768]{1,0:T(8,128)S(1)}, u32[]{:S(2)}, u32[]{:S(2)}) collective-permute-start(f32[48,768]{1,0:T(8,128)S(1)} %get-tuple-element.81.w_ref), channel_id=1, source_target_pairs={{0,8},{8,0},{1,9},{9,1},{2,10},{10,2},{3,11},{11,3},{4,12},{12,4},... | collective-permute-start | bytes 442376 | tf_op jit(solution)/shard_map/ppermute | solution.py:304
  30.9 11.7 %collective-permute-start.13 = (f32[48,768]{1,0:T(8,128)S(1)}, f32[48,768]{1,0:T(8,128)S(1)}, u32[]{:S(2)}, u32[]{:S(2)}) collective-permute-start(f32[48,768]{1,0:T(8,128)S(1)} %get-tuple-element.81.w_ref), channel_id=1, source_target_pairs={{0,1},{1,0},{2,3},{3,2},{4,5},{5,4},{6,7},{7,6},{8,9},{9,8},{10,11... | collective-permute-start | bytes 442376 | tf_op jit(solution)/shard_map/ppermute | solution.py:304
  31.0 11.6 %collective-permute-start.14 = (f32[48,768]{1,0:T(8,128)S(1)}, f32[48,768]{1,0:T(8,128)S(1)}, u32[]{:S(2)}, u32[]{:S(2)}) collective-permute-start(f32[48,768]{1,0:T(8,128)S(1)} %get-tuple-element.81.w_ref), channel_id=1, source_target_pairs={{1,2},{2,1},{3,4},{4,3},{5,6},{6,5},{7,0},{0,7},{9,10},{10,9},{11,... | collective-permute-start | bytes 442376 | tf_op jit(solution)/shard_map/ppermute | solution.py:304
  33.4 4.4 %collective-permute-start.15 = (f32[48,384]{1,0:T(8,128)S(1)}, f32[48,384]{1,0:T(8,128)S(1)}, u32[]{:S(2)}, u32[]{:S(2)}) collective-permute-start(f32[48,384]{1,0:T(8,128)S(1)} %get-tuple-element.84), channel_id=1, source_target_pairs={{0,16},{16,0},{1,17},{17,1},{2,18},{18,2},{3,19},{19,3},{4,20},{20... | collective-permute-start | bytes 221192 | tf_op jit(solution)/shard_map/ppermute | solution.py:304
  34.1 8.5 %collective-permute-start.16 = (f32[48,384]{1,0:T(8,128)S(1)}, f32[48,384]{1,0:T(8,128)S(1)}, u32[]{:S(2)}, u32[]{:S(2)}) collective-permute-start(f32[48,384]{1,0:T(8,128)S(1)} %get-tuple-element.84), channel_id=1, source_target_pairs={{0,17},{17,0},{1,18},{18,1},{2,19},{19,2},{3,20},{20,3},{4,21},{21... | collective-permute-start | bytes 221192 | tf_op jit(solution)/shard_map/ppermute | solution.py:304
  42.9 4.1 %collective-permute-start.17 = (f32[48,768]{1,0:T(8,128)S(1)}, f32[48,768]{1,0:T(8,128)S(1)}, u32[]{:S(2)}, u32[]{:S(2)}) collective-permute-start(f32[48,768]{1,0:T(8,128)S(1)} %get-tuple-element.85.w_ref), channel_id=1, source_target_pairs={{0,8},{8,0},{1,9},{9,1},{2,10},{10,2},{3,11},{11,3},{4,12},{12,4},... | collective-permute-start | bytes 442376 | tf_op jit(solution)/shard_map/ppermute | solution.py:304
  43.0 11.3 %collective-permute-start.18 = (f32[48,768]{1,0:T(8,128)S(1)}, f32[48,768]{1,0:T(8,128)S(1)}, u32[]{:S(2)}, u32[]{:S(2)}) collective-permute-start(f32[48,768]{1,0:T(8,128)S(1)} %get-tuple-element.85.w_ref), channel_id=1, source_target_pairs={{0,1},{1,0},{2,3},{3,2},{4,5},{5,4},{6,7},{7,6},{8,9},{9,8},{10,11... | collective-permute-start | bytes 442376 | tf_op jit(solution)/shard_map/ppermute | solution.py:304
  43.0 11.2 %collective-permute-start.19 = (f32[48,768]{1,0:T(8,128)S(1)}, f32[48,768]{1,0:T(8,128)S(1)}, u32[]{:S(2)}, u32[]{:S(2)}) collective-permute-start(f32[48,768]{1,0:T(8,128)S(1)} %get-tuple-element.85.w_ref), channel_id=1, source_target_pairs={{1,2},{2,1},{3,4},{4,3},{5,6},{6,5},{7,0},{0,7},{9,10},{10,9},{11,... | collective-permute-start | bytes 442376 | tf_op jit(solution)/shard_map/ppermute | solution.py:304
  45.5 4.4 %collective-permute-start.20 = (f32[48,384]{1,0:T(8,128)S(1)}, f32[48,384]{1,0:T(8,128)S(1)}, u32[]{:S(2)}, u32[]{:S(2)}) collective-permute-start(f32[48,384]{1,0:T(8,128)S(1)} %get-tuple-element.88), channel_id=1, source_target_pairs={{0,16},{16,0},{1,17},{17,1},{2,18},{18,2},{3,19},{19,3},{4,20},{20... | collective-permute-start | bytes 221192 | tf_op jit(solution)/shard_map/ppermute | solution.py:304
  46.3 7.9 %collective-permute-start.21 = (f32[48,384]{1,0:T(8,128)S(1)}, f32[48,384]{1,0:T(8,128)S(1)}, u32[]{:S(2)}, u32[]{:S(2)}) collective-permute-start(f32[48,384]{1,0:T(8,128)S(1)} %get-tuple-element.88), channel_id=1, source_target_pairs={{0,17},{17,0},{1,18},{18,1},{2,19},{19,2},{3,20},{20,3},{4,21},{21... | collective-permute-start | bytes 221192 | tf_op jit(solution)/shard_map/ppermute | solution.py:304
  54.5 1.3 %collective-permute-start.22 = (f32[48,384]{1,0:T(8,128)S(1)}, f32[48,384]{1,0:T(8,128)S(1)}, u32[]{:S(2)}, u32[]{:S(2)}) collective-permute-start(f32[48,384]{1,0:T(8,128)S(1)} %get-tuple-element.90), channel_id=1, source_target_pairs={{0,8},{8,0},{1,9},{9,1},{2,10},{10,2},{3,11},{11,3},{4,12},{12,4},... | collective-permute-start | bytes 221192 | tf_op jit(solution)/shard_map/ppermute | solution.py:304
